TPU v7x, 256 devices: a whole 4x4x8 slice. The times are simulated.
256 devices in a mesh: seq: 128 (over x_lo, y, z, core), batch: 2 (over x_hi).
Axes of the slice: x: 4 (x_hi: 2, x_lo: 2; x = x_hi * 2 + x_lo), y: 4, z: 8, core: 2. Of those that a mesh axis runs over, the one named last changes fastest.
Arguments:
- hidden_in: bfloat16 [2, 32768, 2304], P('batch', 'seq'), may hold values from -6 to 6
- segment_ids: int32 [2, 32768], P('batch', 'seq'), may hold values from 0 to 15, never falling along the last dimension, each value on 1 to 4096 neighbouring positions
- pre_gain: float32 [2304], replicated, may hold values from 0.25 to 1.75
- w_qkv: bfloat16 [2304, 2048], P('seq'), may hold values from -0.27083333 to 0.27083333
- w_out: bfloat16 [1024, 2304], P('seq'), may hold values from -0.1875 to 0.1875
- post_gain: float32 [2304], replicated, may hold values from 0.25 to 1.75
Outputs:
- layer_out: bfloat16 [2, 32768, 2304], P('batch', 'seq')
Inputs may be any that keep to these rules, and one draw needn't show every extreme that they name: `segment_ids`: along each sequence the numbers never fall; a document is 1 to 4096 positions long, and each sequence has one of exactly 4096.
All inputs are finite; a program needn't handle non-finite values.
Results may differ from a plain program's by a relative error of at most 0.012.
The roundings to bfloat16 on the way count: a program that leaves them out, or rounds other values in their place, can miss the bound.
Values may be sent and summed in bfloat16 or wider, within the bound.
A program may use at most 128 MiB of HBM per device.

v0:
```python
import math

import jax
import jax.numpy as jnp
from jax import lax
from jax.sharding import PartitionSpec as P

Q_HEADS = 4
KV_HEADS = 2
HEAD = 256
WINDOW = 4096
DOCS = 16


EPS = 1e-06
CAP = 50.0


def over_pieces(x, axis):
    return lax.all_gather(x, axis).min(0)


def from_behind(block, axis, distance):
    devices = range(lax.axis_size(axis))
    route = [(i - distance, i) for i in devices if i - distance in devices]
    return lax.ppermute(block, axis, route)


def rms_scale(values, gain):
    return values * lax.rsqrt(jnp.mean(values * values, axis=-1, keepdims=True) + EPS) * gain


def rotary(values, positions, leading):
    head_size = values.shape[-1]
    half_dim = head_size // 2
    inverse = 1.0 / 10000.0 ** (jnp.arange(half_dim, dtype=jnp.float32) * 2.0 / head_size)
    angles = positions.astype(jnp.float32)[:, None] * inverse[None, :]
    shape = (
        (1,) * leading + (positions.shape[0],) + (1,) * (values.ndim - 2 - leading) + (half_dim,)
    )
    cosine = jnp.cos(angles).reshape(shape)
    sine = jnp.sin(angles).reshape(shape)
    first_half = values[..., :half_dim]
    second_half = values[..., half_dim:]
    return jnp.concatenate(
        [first_half * cosine - second_half * sine, second_half * cosine + first_half * sine],
        axis=-1,
    )


def attend(states, queries, key_block, value_block, query_pos, key_pos, starts):
    running, totals = states
    scores = jnp.einsum(
        "qhgd,khd->qhgk", queries, key_block, preferred_element_type=jnp.float32
    ) * (1.0 / math.sqrt(HEAD))
    capped = CAP * jnp.tanh(scores / CAP)
    allowed = (
        (key_pos[None, :] <= query_pos[:, None])
        & (query_pos[:, None] - key_pos[None, :] < WINDOW)
        & (key_pos[None, :] >= starts[:, None])
    )
    weights = jnp.where(allowed[:, None, None, :], jnp.exp(capped), 0.0)
    totals = totals + jnp.sum(weights, axis=-1)
    running = running + jnp.einsum(
        "qhgk,khd->qhgd",
        weights.astype(jnp.bfloat16),
        value_block,
        preferred_element_type=jnp.float32,
    )
    return (running, totals)


def per_device(hidden_in, segment_ids, pre_gain, w_qkv, w_out, post_gain):
    tok_rows = hidden_in.shape[1]
    seq_count = lax.axis_size("seq")
    seq_index = lax.axis_index("seq")
    groups = Q_HEADS // KV_HEADS
    positions = seq_index * tok_rows + jnp.arange(tok_rows, dtype=jnp.int32)
    widened = hidden_in[0].astype(jnp.float32)
    normed = rms_scale(widened, pre_gain).astype(jnp.bfloat16)
    columns = normed
    projected = jnp.dot(
        columns,
        lax.all_gather(w_qkv, "seq", axis=0, tiled=True),
        preferred_element_type=jnp.float32,
    )
    queries = rotary(
        projected[:, : Q_HEADS * HEAD].reshape(tok_rows, KV_HEADS, groups, HEAD), positions, 0
    ).astype(jnp.bfloat16)
    key_rows = rotary(
        projected[:, Q_HEADS * HEAD : (Q_HEADS + KV_HEADS) * HEAD].reshape(
            tok_rows, KV_HEADS, HEAD
        ),
        positions,
        0,
    ).astype(jnp.bfloat16)
    value_rows = (
        projected[:, (Q_HEADS + KV_HEADS) * HEAD :]
        .reshape(tok_rows, KV_HEADS, HEAD)
        .astype(jnp.bfloat16)
    )
    doc_numbers = jnp.arange(DOCS, dtype=jnp.int32)
    matches = segment_ids[0][:, None] == doc_numbers[None, :]
    local_first = jnp.min(jnp.where(matches, positions[:, None], seq_count * tok_rows), axis=0)
    first_pos = over_pieces(local_first, "seq")
    starts = jnp.sum(jnp.where(matches, first_pos[None, :], 0), axis=1)
    states = (
        jnp.zeros((tok_rows, KV_HEADS, groups, HEAD), jnp.float32),
        jnp.zeros((tok_rows, KV_HEADS, groups), jnp.float32),
    )
    states = attend(states, queries, key_rows, value_rows, positions, positions, starts)
    hop_count = min(WINDOW // tok_rows, seq_count - 1)

    def relay_step(hop_index, carried):
        moving_keys, moving_values, running, totals = carried
        moving_keys, moving_values = from_behind((moving_keys, moving_values), "seq", 1)
        running, totals = attend(
            (running, totals),
            queries,
            moving_keys,
            moving_values,
            positions,
            positions - hop_index * tok_rows,
            starts,
        )
        return (moving_keys, moving_values, running, totals)

    carried = lax.fori_loop(
        1, hop_count + 1, relay_step, (key_rows, value_rows, states[0], states[1])
    )
    states = (carried[2], carried[3])
    running, totals = states
    attended = (running / totals[..., None]).astype(jnp.bfloat16).reshape(tok_rows, Q_HEADS * HEAD)
    columns = attended
    branch = jnp.dot(
        columns,
        lax.all_gather(w_out, "seq", axis=0, tiled=True),
        preferred_element_type=jnp.float32,
    )
    return (widened + rms_scale(branch, post_gain)).astype(jnp.bfloat16)[None]


def solution(mesh):
    placed = (P("batch", "seq", None), P("batch", "seq"), P(), P("seq", None), P("seq", None), P())
    return jax.shard_map(
        per_device, mesh=mesh, in_specs=placed, out_specs=P("batch", "seq", None), check_vma=False
    )
```

profile of v0, /device:TPU:6, one launch (start us, length us, event | category | flops | bytes accessed | tf_op | source)
XLA Modules:
  0.0 526.2 jit_solution(17431451830211270644)
XLA Ops:
  12.6 26.9 %all-reduce = s32[2048]{0:T(1024)S(1)} all-reduce(s32[2048]{0:T(1024)S(1)} %dynamic-update-slice), channel_id=2, replica_groups=mesh['seq'=128,'batch'=2] {'seq'}, use_global_device_ids=true, to_apply=%add | all-reduce | flops 2048 | bytes 16384
  42.4 194.4 %all-gather.7.cloned.1.call-done = bf16[128,18,2048]{2,1,0:T(8,128)(2,1)} async-done(((bf16[1,18,2048]{2,1,0:T(8,128)(2,1)}), bf16[128,18,2048]{2,1,0:T(8,128)(2,1)}) %all-gather.7.cloned.1.call-update) | async-done | bytes 9437200 | tf_op jit(solution)/shard_map/all_gather | solution.py:84
  236.8 14.1 %reshape.315 = bf16[2304,2048]{1,0:T(8,128)(2,1)} reshape(bf16[128,18,2048]{2,1,0:T(8,128)(2,1)} %all-gather.7.cloned.1.call-done) | data formatting | bytes 18874368
  250.8 5.3 %fusion.23 = f32[256,2048]{1,0:T(8,128)S(1)} fusion(bf16[2304,2048]{1,0:T(8,128)(2,1)} %reshape.315, bf16[1,256,2304]{2,1,0:T(8,128)(2,1)S(1)} %copy-done, f32[2304]{0:T(1024)S(1)} %copy-done.7, f32[256]{0:T(256)S(1)} %add_rsqrt_fusion.1), kind=kOutput, calls=%fused_computation.33 | convolution fusion | flops 2418278400 | bytes 12724224 | tf_op jit(solution)/shard_map/dot_general | solution.py:82
  264.7 248.8 %while.22 = (s32[]{:T(128)}, bf16[256,2,256]{2,0,1:T(8,128)(2,1)}, bf16[256,2,256]{2,0,1:T(8,128)(2,1)S(1)}, f32[256,2,2,256]{3,0,2,1:T(8,128)S(1)}, f32[256,2,2...) while((s32[]{:T(128)}, bf16[256,2,256]{2,0,1:T(8,128)(2,1)}, ...), condition=%wide.region_7.8_spmd.clone, body=%wide.region_5.7_spmd.clone.sunk | while | flops 270402048 | bytes 7492809 | solution.py:128
  266.6 1.9 collective-permute-start.1
  268.7 8.2 %collective-permute-done = bf16[256,2,256]{2,0,1:T(8,128)(2,1)S(1)} collective-permute-done((bf16[256,2,256]{2,0,1:T(8,128)(2,1)}, bf16[256,2,256]{2,0,1:T(8,128)(2,1)S(1)}, u32[]{:S(2)}, u32[]{:S(2)}) %collective-permute-start) | collective-permute-done | bytes 262176 | tf_op jit(solution)/shard_map/while/body/eval_jaxpr/ppermute | solution.py:26
  282.2 1.9 collective-permute-start.1
  284.3 8.1 %collective-permute-done = bf16[256,2,256]{2,0,1:T(8,128)(2,1)S(1)} collective-permute-done((bf16[256,2,256]{2,0,1:T(8,128)(2,1)}, bf16[256,2,256]{2,0,1:T(8,128)(2,1)S(1)}, u32[]{:S(2)}, u32[]{:S(2)}) %collective-permute-start) | collective-permute-done | bytes 262176 | tf_op jit(solution)/shard_map/while/body/eval_jaxpr/ppermute | solution.py:26
  299.8 8.2 %collective-permute-done = bf16[256,2,256]{2,0,1:T(8,128)(2,1)S(1)} collective-permute-done((bf16[256,2,256]{2,0,1:T(8,128)(2,1)}, bf16[256,2,256]{2,0,1:T(8,128)(2,1)S(1)}, u32[]{:S(2)}, u32[]{:S(2)}) %collective-permute-start) | collective-permute-done | bytes 262176 | tf_op jit(solution)/shard_map/while/body/eval_jaxpr/ppermute | solution.py:26
  315.4 8.2 %collective-permute-done = bf16[256,2,256]{2,0,1:T(8,128)(2,1)S(1)} collective-permute-done((bf16[256,2,256]{2,0,1:T(8,128)(2,1)}, bf16[256,2,256]{2,0,1:T(8,128)(2,1)S(1)}, u32[]{:S(2)}, u32[]{:S(2)}) %collective-permute-start) | collective-permute-done | bytes 262176 | tf_op jit(solution)/shard_map/while/body/eval_jaxpr/ppermute | solution.py:26
  331.0 8.2 %collective-permute-done = bf16[256,2,256]{2,0,1:T(8,128)(2,1)S(1)} collective-permute-done((bf16[256,2,256]{2,0,1:T(8,128)(2,1)}, bf16[256,2,256]{2,0,1:T(8,128)(2,1)S(1)}, u32[]{:S(2)}, u32[]{:S(2)}) %collective-permute-start) | collective-permute-done | bytes 262176 | tf_op jit(solution)/shard_map/while/body/eval_jaxpr/ppermute | solution.py:26
  346.5 8.2 %collective-permute-done = bf16[256,2,256]{2,0,1:T(8,128)(2,1)S(1)} collective-permute-done((bf16[256,2,256]{2,0,1:T(8,128)(2,1)}, bf16[256,2,256]{2,0,1:T(8,128)(2,1)S(1)}, u32[]{:S(2)}, u32[]{:S(2)}) %collective-permute-start) | collective-permute-done | bytes 262176 | tf_op jit(solution)/shard_map/while/body/eval_jaxpr/ppermute | solution.py:26
  362.1 8.1 %collective-permute-done = bf16[256,2,256]{2,0,1:T(8,128)(2,1)S(1)} collective-permute-done((bf16[256,2,256]{2,0,1:T(8,128)(2,1)}, bf16[256,2,256]{2,0,1:T(8,128)(2,1)S(1)}, u32[]{:S(2)}, u32[]{:S(2)}) %collective-permute-start) | collective-permute-done | bytes 262176 | tf_op jit(solution)/shard_map/while/body/eval_jaxpr/ppermute | solution.py:26
  377.6 8.1 %collective-permute-done = bf16[256,2,256]{2,0,1:T(8,128)(2,1)S(1)} collective-permute-done((bf16[256,2,256]{2,0,1:T(8,128)(2,1)}, bf16[256,2,256]{2,0,1:T(8,128)(2,1)S(1)}, u32[]{:S(2)}, u32[]{:S(2)}) %collective-permute-start) | collective-permute-done | bytes 262176 | tf_op jit(solution)/shard_map/while/body/eval_jaxpr/ppermute | solution.py:26
  393.2 8.2 %collective-permute-done = bf16[256,2,256]{2,0,1:T(8,128)(2,1)S(1)} collective-permute-done((bf16[256,2,256]{2,0,1:T(8,128)(2,1)}, bf16[256,2,256]{2,0,1:T(8,128)(2,1)S(1)}, u32[]{:S(2)}, u32[]{:S(2)}) %collective-permute-start) | collective-permute-done | bytes 262176 | tf_op jit(solution)/shard_map/while/body/eval_jaxpr/ppermute | solution.py:26
  408.7 8.2 %collective-permute-done = bf16[256,2,256]{2,0,1:T(8,128)(2,1)S(1)} collective-permute-done((bf16[256,2,256]{2,0,1:T(8,128)(2,1)}, bf16[256,2,256]{2,0,1:T(8,128)(2,1)S(1)}, u32[]{:S(2)}, u32[]{:S(2)}) %collective-permute-start) | collective-permute-done | bytes 262176 | tf_op jit(solution)/shard_map/while/body/eval_jaxpr/ppermute | solution.py:26
  424.3 8.2 %collective-permute-done = bf16[256,2,256]{2,0,1:T(8,128)(2,1)S(1)} collective-permute-done((bf16[256,2,256]{2,0,1:T(8,128)(2,1)}, bf16[256,2,256]{2,0,1:T(8,128)(2,1)S(1)}, u32[]{:S(2)}, u32[]{:S(2)}) %collective-permute-start) | collective-permute-done | bytes 262176 | tf_op jit(solution)/shard_map/while/body/eval_jaxpr/ppermute | solution.py:26
  439.8 8.2 %collective-permute-done = bf16[256,2,256]{2,0,1:T(8,128)(2,1)S(1)} collective-permute-done((bf16[256,2,256]{2,0,1:T(8,128)(2,1)}, bf16[256,2,256]{2,0,1:T(8,128)(2,1)S(1)}, u32[]{:S(2)}, u32[]{:S(2)}) %collective-permute-start) | collective-permute-done | bytes 262176 | tf_op jit(solution)/shard_map/while/body/eval_jaxpr/ppermute | solution.py:26
  455.4 8.2 %collective-permute-done = bf16[256,2,256]{2,0,1:T(8,128)(2,1)S(1)} collective-permute-done((bf16[256,2,256]{2,0,1:T(8,128)(2,1)}, bf16[256,2,256]{2,0,1:T(8,128)(2,1)S(1)}, u32[]{:S(2)}, u32[]{:S(2)}) %collective-permute-start) | collective-permute-done | bytes 262176 | tf_op jit(solution)/shard_map/while/body/eval_jaxpr/ppermute | solution.py:26
  471.0 8.2 %collective-permute-done = bf16[256,2,256]{2,0,1:T(8,128)(2,1)S(1)} collective-permute-done((bf16[256,2,256]{2,0,1:T(8,128)(2,1)}, bf16[256,2,256]{2,0,1:T(8,128)(2,1)S(1)}, u32[]{:S(2)}, u32[]{:S(2)}) %collective-permute-start) | collective-permute-done | bytes 262176 | tf_op jit(solution)/shard_map/while/body/eval_jaxpr/ppermute | solution.py:26
  486.5 8.2 %collective-permute-done = bf16[256,2,256]{2,0,1:T(8,128)(2,1)S(1)} collective-permute-done((bf16[256,2,256]{2,0,1:T(8,128)(2,1)}, bf16[256,2,256]{2,0,1:T(8,128)(2,1)S(1)}, u32[]{:S(2)}, u32[]{:S(2)}) %collective-permute-start) | collective-permute-done | bytes 262176 | tf_op jit(solution)/shard_map/while/body/eval_jaxpr/ppermute | solution.py:26
  502.1 8.1 %collective-permute-done = bf16[256,2,256]{2,0,1:T(8,128)(2,1)S(1)} collective-permute-done((bf16[256,2,256]{2,0,1:T(8,128)(2,1)}, bf16[256,2,256]{2,0,1:T(8,128)(2,1)S(1)}, u32[]{:S(2)}, u32[]{:S(2)}) %collective-permute-start) | collective-permute-done | bytes 262176 | tf_op jit(solution)/shard_map/while/body/eval_jaxpr/ppermute | solution.py:26
  514.0 3.9 multiply_reduce_fusion
  (212 shorter events, 131.8 us)
Async XLA Ops:
  6.5 230.2 %all-gather.7.cloned.1.call-start = ((), (), s32[]{:S(2)}) async-start(), calls=%async_computation.1 | async-start | bytes 12681216 | tf_op jit(solution)/shard_map/all_gather | solution.py:84
  7.3 506.7 %all-gather.5.cloned.1.call-start = ((), (), s32[]{:S(2)}) async-start(), calls=%async_computation | async-start | bytes 4755456 | tf_op jit(solution)/shard_map/all_gather | solution.py:137
  266.6 13.1 %collective-permute-start.1 = (bf16[256,2,256]{2,0,1:T(8,128)(2,1)S(1)}, bf16[256,2,256]{2,0,1:T(8,128)(2,1)S(1)}, u32[]{:S(2)}, u32[]{:S(2)}) collective-permute-start(bf16[256,2,256]{2,0,1:T(8,128)(2,1)S(1)} %get-tuple-element.366), channel_id=1, source_target_pairs={{0,2},{2,4},{4,6},{6,8},{8,10},{10,12},{12,14},{14,16},{16,18},{18... | collective-permute-start | bytes 786440 | tf_op jit(solution)/shard_map/while/body/eval_jaxpr/ppermute | solution.py:26
  282.2 13.1 %collective-permute-start.1 = (bf16[256,2,256]{2,0,1:T(8,128)(2,1)S(1)}, bf16[256,2,256]{2,0,1:T(8,128)(2,1)S(1)}, u32[]{:S(2)}, u32[]{:S(2)}) collective-permute-start(bf16[256,2,256]{2,0,1:T(8,128)(2,1)S(1)} %get-tuple-element.366), channel_id=1, source_target_pairs={{0,2},{2,4},{4,6},{6,8},{8,10},{10,12},{12,14},{14,16},{16,18},{18... | collective-permute-start | bytes 786440 | tf_op jit(solution)/shard_map/while/body/eval_jaxpr/ppermute | solution.py:26
  295.8 12.2 %collective-permute-start = (bf16[256,2,256]{2,0,1:T(8,128)(2,1)}, bf16[256,2,256]{2,0,1:T(8,128)(2,1)S(1)}, u32[]{:S(2)}, u32[]{:S(2)}) collective-permute-start(bf16[256,2,256]{2,0,1:T(8,128)(2,1)} %get-tuple-element.365), channel_id=1, source_target_pairs={{0,2},{2,4},{4,6},{6,8},{8,10},{10,12},{12,14},{14,16},{16,18},{18... | collective-permute-start | bytes 786440 | tf_op jit(solution)/shard_map/while/body/eval_jaxpr/ppermute | solution.py:26
  297.7 13.1 %collective-permute-start.1 = (bf16[256,2,256]{2,0,1:T(8,128)(2,1)S(1)}, bf16[256,2,256]{2,0,1:T(8,128)(2,1)S(1)}, u32[]{:S(2)}, u32[]{:S(2)}) collective-permute-start(bf16[256,2,256]{2,0,1:T(8,128)(2,1)S(1)} %get-tuple-element.366), channel_id=1, source_target_pairs={{0,2},{2,4},{4,6},{6,8},{8,10},{10,12},{12,14},{14,16},{16,18},{18... | collective-permute-start | bytes 786440 | tf_op jit(solution)/shard_map/while/body/eval_jaxpr/ppermute | solution.py:26
  311.4 12.2 %collective-permute-start = (bf16[256,2,256]{2,0,1:T(8,128)(2,1)}, bf16[256,2,256]{2,0,1:T(8,128)(2,1)S(1)}, u32[]{:S(2)}, u32[]{:S(2)}) collective-permute-start(bf16[256,2,256]{2,0,1:T(8,128)(2,1)} %get-tuple-element.365), channel_id=1, source_target_pairs={{0,2},{2,4},{4,6},{6,8},{8,10},{10,12},{12,14},{14,16},{16,18},{18... | collective-permute-start | bytes 786440 | tf_op jit(solution)/shard_map/while/body/eval_jaxpr/ppermute | solution.py:26
  313.3 13.1 %collective-permute-start.1 = (bf16[256,2,256]{2,0,1:T(8,128)(2,1)S(1)}, bf16[256,2,256]{2,0,1:T(8,128)(2,1)S(1)}, u32[]{:S(2)}, u32[]{:S(2)}) collective-permute-start(bf16[256,2,256]{2,0,1:T(8,128)(2,1)S(1)} %get-tuple-element.366), channel_id=1, source_target_pairs={{0,2},{2,4},{4,6},{6,8},{8,10},{10,12},{12,14},{14,16},{16,18},{18... | collective-permute-start | bytes 786440 | tf_op jit(solution)/shard_map/while/body/eval_jaxpr/ppermute | solution.py:26
  326.9 12.2 %collective-permute-start = (bf16[256,2,256]{2,0,1:T(8,128)(2,1)}, bf16[256,2,256]{2,0,1:T(8,128)(2,1)S(1)}, u32[]{:S(2)}, u32[]{:S(2)}) collective-permute-start(bf16[256,2,256]{2,0,1:T(8,128)(2,1)} %get-tuple-element.365), channel_id=1, source_target_pairs={{0,2},{2,4},{4,6},{6,8},{8,10},{10,12},{12,14},{14,16},{16,18},{18... | collective-permute-start | bytes 786440 | tf_op jit(solution)/shard_map/while/body/eval_jaxpr/ppermute | solution.py:26
  328.9 13.1 %collective-permute-start.1 = (bf16[256,2,256]{2,0,1:T(8,128)(2,1)S(1)}, bf16[256,2,256]{2,0,1:T(8,128)(2,1)S(1)}, u32[]{:S(2)}, u32[]{:S(2)}) collective-permute-start(bf16[256,2,256]{2,0,1:T(8,128)(2,1)S(1)} %get-tuple-element.366), channel_id=1, source_target_pairs={{0,2},{2,4},{4,6},{6,8},{8,10},{10,12},{12,14},{14,16},{16,18},{18... | collective-permute-start | bytes 786440 | tf_op jit(solution)/shard_map/while/body/eval_jaxpr/ppermute | solution.py:26
  342.5 12.2 %collective-permute-start = (bf16[256,2,256]{2,0,1:T(8,128)(2,1)}, bf16[256,2,256]{2,0,1:T(8,128)(2,1)S(1)}, u32[]{:S(2)}, u32[]{:S(2)}) collective-permute-start(bf16[256,2,256]{2,0,1:T(8,128)(2,1)} %get-tuple-element.365), channel_id=1, source_target_pairs={{0,2},{2,4},{4,6},{6,8},{8,10},{10,12},{12,14},{14,16},{16,18},{18... | collective-permute-start | bytes 786440 | tf_op jit(solution)/shard_map/while/body/eval_jaxpr/ppermute | solution.py:26
  344.4 13.1 %collective-permute-start.1 = (bf16[256,2,256]{2,0,1:T(8,128)(2,1)S(1)}, bf16[256,2,256]{2,0,1:T(8,128)(2,1)S(1)}, u32[]{:S(2)}, u32[]{:S(2)}) collective-permute-start(bf16[256,2,256]{2,0,1:T(8,128)(2,1)S(1)} %get-tuple-element.366), channel_id=1, source_target_pairs={{0,2},{2,4},{4,6},{6,8},{8,10},{10,12},{12,14},{14,16},{16,18},{18... | collective-permute-start | bytes 786440 | tf_op jit(solution)/shard_map/while/body/eval_jaxpr/ppermute | solution.py:26
  360.0 13.1 %collective-permute-start.1 = (bf16[256,2,256]{2,0,1:T(8,128)(2,1)S(1)}, bf16[256,2,256]{2,0,1:T(8,128)(2,1)S(1)}, u32[]{:S(2)}, u32[]{:S(2)}) collective-permute-start(bf16[256,2,256]{2,0,1:T(8,128)(2,1)S(1)} %get-tuple-element.366), channel_id=1, source_target_pairs={{0,2},{2,4},{4,6},{6,8},{8,10},{10,12},{12,14},{14,16},{16,18},{18... | collective-permute-start | bytes 786440 | tf_op jit(solution)/shard_map/while/body/eval_jaxpr/ppermute | solution.py:26
  375.5 13.1 %collective-permute-start.1 = (bf16[256,2,256]{2,0,1:T(8,128)(2,1)S(1)}, bf16[256,2,256]{2,0,1:T(8,128)(2,1)S(1)}, u32[]{:S(2)}, u32[]{:S(2)}) collective-permute-start(bf16[256,2,256]{2,0,1:T(8,128)(2,1)S(1)} %get-tuple-element.366), channel_id=1, source_target_pairs={{0,2},{2,4},{4,6},{6,8},{8,10},{10,12},{12,14},{14,16},{16,18},{18... | collective-permute-start | bytes 786440 | tf_op jit(solution)/shard_map/while/body/eval_jaxpr/ppermute | solution.py:26
  391.1 13.1 %collective-permute-start.1 = (bf16[256,2,256]{2,0,1:T(8,128)(2,1)S(1)}, bf16[256,2,256]{2,0,1:T(8,128)(2,1)S(1)}, u32[]{:S(2)}, u32[]{:S(2)}) collective-permute-start(bf16[256,2,256]{2,0,1:T(8,128)(2,1)S(1)} %get-tuple-element.366), channel_id=1, source_target_pairs={{0,2},{2,4},{4,6},{6,8},{8,10},{10,12},{12,14},{14,16},{16,18},{18... | collective-permute-start | bytes 786440 | tf_op jit(solution)/shard_map/while/body/eval_jaxpr/ppermute | solution.py:26
  404.7 12.2 %collective-permute-start = (bf16[256,2,256]{2,0,1:T(8,128)(2,1)}, bf16[256,2,256]{2,0,1:T(8,128)(2,1)S(1)}, u32[]{:S(2)}, u32[]{:S(2)}) collective-permute-start(bf16[256,2,256]{2,0,1:T(8,128)(2,1)} %get-tuple-element.365), channel_id=1, source_target_pairs={{0,2},{2,4},{4,6},{6,8},{8,10},{10,12},{12,14},{14,16},{16,18},{18... | collective-permute-start | bytes 786440 | tf_op jit(solution)/shard_map/while/body/eval_jaxpr/ppermute | solution.py:26
  406.6 13.1 %collective-permute-start.1 = (bf16[256,2,256]{2,0,1:T(8,128)(2,1)S(1)}, bf16[256,2,256]{2,0,1:T(8,128)(2,1)S(1)}, u32[]{:S(2)}, u32[]{:S(2)}) collective-permute-start(bf16[256,2,256]{2,0,1:T(8,128)(2,1)S(1)} %get-tuple-element.366), channel_id=1, source_target_pairs={{0,2},{2,4},{4,6},{6,8},{8,10},{10,12},{12,14},{14,16},{16,18},{18... | collective-permute-start | bytes 786440 | tf_op jit(solution)/shard_map/while/body/eval_jaxpr/ppermute | solution.py:26
  422.2 13.1 %collective-permute-start.1 = (bf16[256,2,256]{2,0,1:T(8,128)(2,1)S(1)}, bf16[256,2,256]{2,0,1:T(8,128)(2,1)S(1)}, u32[]{:S(2)}, u32[]{:S(2)}) collective-permute-start(bf16[256,2,256]{2,0,1:T(8,128)(2,1)S(1)} %get-tuple-element.366), channel_id=1, source_target_pairs={{0,2},{2,4},{4,6},{6,8},{8,10},{10,12},{12,14},{14,16},{16,18},{18... | collective-permute-start | bytes 786440 | tf_op jit(solution)/shard_map/while/body/eval_jaxpr/ppermute | solution.py:26
  435.8 12.2 %collective-permute-start = (bf16[256,2,256]{2,0,1:T(8,128)(2,1)}, bf16[256,2,256]{2,0,1:T(8,128)(2,1)S(1)}, u32[]{:S(2)}, u32[]{:S(2)}) collective-permute-start(bf16[256,2,256]{2,0,1:T(8,128)(2,1)} %get-tuple-element.365), channel_id=1, source_target_pairs={{0,2},{2,4},{4,6},{6,8},{8,10},{10,12},{12,14},{14,16},{16,18},{18... | collective-permute-start | bytes 786440 | tf_op jit(solution)/shard_map/while/body/eval_jaxpr/ppermute | solution.py:26
  437.7 13.1 %collective-permute-start.1 = (bf16[256,2,256]{2,0,1:T(8,128)(2,1)S(1)}, bf16[256,2,256]{2,0,1:T(8,128)(2,1)S(1)}, u32[]{:S(2)}, u32[]{:S(2)}) collective-permute-start(bf16[256,2,256]{2,0,1:T(8,128)(2,1)S(1)} %get-tuple-element.366), channel_id=1, source_target_pairs={{0,2},{2,4},{4,6},{6,8},{8,10},{10,12},{12,14},{14,16},{16,18},{18... | collective-permute-start | bytes 786440 | tf_op jit(solution)/shard_map/while/body/eval_jaxpr/ppermute | solution.py:26
  453.3 13.1 %collective-permute-start.1 = (bf16[256,2,256]{2,0,1:T(8,128)(2,1)S(1)}, bf16[256,2,256]{2,0,1:T(8,128)(2,1)S(1)}, u32[]{:S(2)}, u32[]{:S(2)}) collective-permute-start(bf16[256,2,256]{2,0,1:T(8,128)(2,1)S(1)} %get-tuple-element.366), channel_id=1, source_target_pairs={{0,2},{2,4},{4,6},{6,8},{8,10},{10,12},{12,14},{14,16},{16,18},{18... | collective-permute-start | bytes 786440 | tf_op jit(solution)/shard_map/while/body/eval_jaxpr/ppermute | solution.py:26
  468.9 13.1 %collective-permute-start.1 = (bf16[256,2,256]{2,0,1:T(8,128)(2,1)S(1)}, bf16[256,2,256]{2,0,1:T(8,128)(2,1)S(1)}, u32[]{:S(2)}, u32[]{:S(2)}) collective-permute-start(bf16[256,2,256]{2,0,1:T(8,128)(2,1)S(1)} %get-tuple-element.366), channel_id=1, source_target_pairs={{0,2},{2,4},{4,6},{6,8},{8,10},{10,12},{12,14},{14,16},{16,18},{18... | collective-permute-start | bytes 786440 | tf_op jit(solution)/shard_map/while/body/eval_jaxpr/ppermute | solution.py:26
  484.4 13.1 %collective-permute-start.1 = (bf16[256,2,256]{2,0,1:T(8,128)(2,1)S(1)}, bf16[256,2,256]{2,0,1:T(8,128)(2,1)S(1)}, u32[]{:S(2)}, u32[]{:S(2)}) collective-permute-start(bf16[256,2,256]{2,0,1:T(8,128)(2,1)S(1)} %get-tuple-element.366), channel_id=1, source_target_pairs={{0,2},{2,4},{4,6},{6,8},{8,10},{10,12},{12,14},{14,16},{16,18},{18... | collective-permute-start | bytes 786440 | tf_op jit(solution)/shard_map/while/body/eval_jaxpr/ppermute | solution.py:26
  500.0 13.0 %collective-permute-start.1 = (bf16[256,2,256]{2,0,1:T(8,128)(2,1)S(1)}, bf16[256,2,256]{2,0,1:T(8,128)(2,1)S(1)}, u32[]{:S(2)}, u32[]{:S(2)}) collective-permute-start(bf16[256,2,256]{2,0,1:T(8,128)(2,1)S(1)} %get-tuple-element.366), channel_id=1, source_target_pairs={{0,2},{2,4},{4,6},{6,8},{8,10},{10,12},{12,14},{14,16},{16,18},{18... | collective-permute-start | bytes 786440 | tf_op jit(solution)/shard_map/while/body/eval_jaxpr/ppermute | solution.py:26
  (18 other events, 551.9 us)
Sparse Core Ops, SparseCore 0:
  9.2 227.5 all-gather.6
  238.6 259.9 all-gather.4
where the time goes:
time: 529 us; the launch traced here: 526 us
  waiting for transfers between devices  335 us (63%)
  starting transfers between devices  61.5 us (12%)
  matrix products  42.9 us (8%)
  local copies, waits for them, and re-layouts  32.1 us (6%)
  blocking collectives  26.9 us (5%)
  between operations  14.3 us (3%)
  other arithmetic  12.2 us (2%)
    all_gather x1, waiting for transfers between devices, per_device(): lax.all_gather(w_qkv, 'seq', axis=0, tiled=True)  194 us
    ppermute x32, waiting for transfers between devices, from_behind(): return lax.ppermute(block, axis, route)  139 us
    ppermute x32, starting transfers between devices, from_behind(): return lax.ppermute(block, axis, route)  61.4 us
    unnamed x1, blocking collectives  26.9 us
    dot_general x17, matrix products, attend(): jnp.einsum('qhgd,khd->qhgk', queries, key_block, preferred_element_type=j...  25.6 us
    unnamed x21, local copies, waits for them, and re-layouts  16.2 us
    while x32, local copies, waits for them, and re-layouts  11.4 us
  transfers between devices with their start and end apart: 34, of which 33 were waited for; matrix products, arithmetic and copies ran while one was open for 16% of the time, Pallas kernels for 0%

commit v1 on v0

v1 whole, which is shorter than its diff:
```python
import jax
import jax.numpy as jnp
from jax import lax
from jax.experimental import pallas as pl
from jax.experimental.pallas import tpu as pltpu
from jax.sharding import PartitionSpec as P

MESH = pl.DeviceIdType.MESH
BF, F32, I32 = jnp.bfloat16, jnp.float32, jnp.int32

D = 2304
HEAD = 256
WINDOW = 4096
TOK = 256
CHIP = 512
SEQ_DEV = 128
LINES = 8
LROWS = 288
OROWS = 128
EPS = 1e-06
CAP = 50.0
LOG2E = 1.4426950408889634


def kernel(
    hid, seg, wqkv, wout, cos, sin, pre, post, out,
    H, N, W, WO, ZW, ZQ, ZO, FS, ACC, QQ, O, L, A, B, SEGW, QS, ATT, SB, BR,
    s_loc, s_z, r_z, s_s, r_s, s_y, r_y, s_x, r_x, s_a, r_a, s_b, r_b, s_m, r_m,
):
    seq = lax.axis_index("seq")
    bat = lax.axis_index("batch")
    core = lax.rem(seq, 2)
    other = 1 - core
    me = lax.rem(seq, 16)
    z = lax.div(me, 2)
    line = lax.div(seq, 16)
    y = lax.rem(line, 4)
    xl = lax.div(line, 4)

    def dev(s, b=bat):
        return {"seq": s, "batch": b}

    def at_line(xx, yy):
        return (xx * 4 + yy) * 16 + me

    yp, ym, y2 = lax.rem(y + 1, 4), lax.rem(y + 3, 4), lax.rem(y + 2, 4)
    up, down = dev(at_line(xl, yp)), dev(at_line(xl, ym))
    x0, x1 = dev(at_line(1 - xl, y)), dev(at_line(1 - xl, y), 1 - bat)
    nxt, prv = dev(lax.rem(seq + 2, SEQ_DEV)), dev(lax.rem(seq + 126, SEQ_DEV))
    nxt8, prv8 = dev(lax.rem(seq + 16, SEQ_DEV)), dev(lax.rem(seq + 112, SEQ_DEV))
    mate = dev(seq + 1 - 2 * core)

    def z_dev(d, c):
        return dev(line * 16 + lax.rem(z + d, 8) * 2 + c)

    def rc(src, dst, ss, rs, to):
        return pltpu.make_async_remote_copy(
            src_ref=src, dst_ref=dst, send_sem=ss, recv_sem=rs, device_id=to, device_id_type=MESH
        )

    def got(ref, rs):
        rc(ref, ref, s_m.at[0], rs, mate).wait_recv()

    sends = []

    def send(src, dst, ss, rs, to):
        copy = rc(src, dst, ss, rs, to)
        copy.start()
        sends.append(copy)

    barrier = pltpu.get_barrier_semaphore()

    def greet(to):
        pl.semaphore_signal(barrier, inc=1, device_id=to, device_id_type=MESH)

    @pl.loop(1, 8)
    def _(d):
        greet(z_dev(d, 0))
        greet(z_dev(d, 1))

    for to in (mate, up, down, x0, x1, nxt, prv, nxt8, prv8):
        greet(to)

    own = pl.ds(pl.multiple_of(core * TOK, TOK), TOK)
    local = [
        pltpu.make_async_copy(hid, H.at[own], s_loc.at[0]),
        pltpu.make_async_copy(
            wqkv.at[:, pl.ds(pl.multiple_of(1024 + 256 * core, 256), 256)],
            ZW.at[me, :, pl.ds(0, 256)],
            s_loc.at[1],
        ),
        pltpu.make_async_copy(
            wqkv.at[:, pl.ds(pl.multiple_of(1536 + 256 * core, 256), 256)],
            ZW.at[me, :, pl.ds(256, 256)],
            s_loc.at[2],
        ),
        pltpu.make_async_copy(
            wqkv.at[:, pl.ds(pl.multiple_of(512 * core, 512), 512)], ZQ.at[me], s_loc.at[3]
        ),
        pltpu.make_async_copy(
            wout.at[:, pl.ds(pl.multiple_of(1152 * core, 128), 1152)], ZO.at[me], s_loc.at[4]
        ),
        pltpu.make_async_copy(seg, SEGW.at[16 + me], s_loc.at[5]),
    ]
    for copy in local:
        copy.start()

    pl.semaphore_wait(barrier, 23)

    def z_copies(p, slot, c, to):
        if p == 0:
            src, dst = wqkv.at[:, pl.ds(pl.multiple_of(1024 + 256 * c, 256), 256)], ZW.at[me, :, pl.ds(0, 256)]
        elif p == 1:
            src, dst = wqkv.at[:, pl.ds(pl.multiple_of(1536 + 256 * c, 256), 256)], ZW.at[me, :, pl.ds(256, 256)]
        elif p == 2:
            src, dst = wqkv.at[:, pl.ds(pl.multiple_of(512 * c, 512), 512)], ZQ.at[me]
        else:
            src, dst = wout.at[:, pl.ds(pl.multiple_of(1152 * c, 128), 1152)], ZO.at[me]
        return rc(src, dst, s_z.at[p, slot], r_z.at[p, me], to)

    def z_send(*pieces):
        @pl.loop(1, 8)
        def _(d):
            for c in (0, 1):
                for p in pieces:
                    z_copies(p, 2 * d + c, c, z_dev(d, c)).start()

        for p in pieces:
            z_copies(p, 0, other, mate).start()

    def z_landing(p, i):
        if p == 0:
            return ZW.at[i, :, pl.ds(0, 256)]
        if p == 1:
            return ZW.at[i, :, pl.ds(256, 256)]
        return ZQ.at[i] if p == 2 else ZO.at[i]

    def z_got(*pieces):
        @pl.loop(1, 16)
        def _(i):
            j = lax.rem(me + i, 16)
            for p in pieces:
                got(z_landing(p, j), r_z.at[p, j])

    def seg_copy(slot, to):
        return rc(seg, SEGW.at[16 + me], s_s.at[slot], r_s.at[me], to)

    z_send(0, 1)
    send(hid, H.at[own], s_m.at[1], r_m.at[1], mate)

    @pl.loop(1, 8)
    def _(d):
        for c in (0, 1):
            seg_copy(2 * d + c, z_dev(d, c)).start()

    seg_copy(0, mate).start()
    z_send(2)
    z_send(3)

    def norm_rows(first):
        @pl.loop(0, TOK // 64)
        def _(i):
            rows = pl.ds(pl.multiple_of(first + i * 64, 64), 64)
            v = H[rows, :].astype(F32)
            v = v * lax.rsqrt(jnp.mean(v * v, axis=-1, keepdims=True) + EPS) * pre[...]
            v = v.astype(BF)
            N[0, rows, :] = v[:, : D // 2]
            N[1, rows, :] = v[:, D // 2 :]

    local[0].wait()
    norm_rows(core * TOK)
    theirs = pl.ds(pl.multiple_of(other * TOK, TOK), TOK)
    got(H.at[theirs], r_m.at[1])
    norm_rows(other * TOK)

    def part(s, yy, half, xx=xl):
        ln = xx * 4 + yy
        n = OROWS if s == 2 else LROWS
        first, size = (0, n) if half is None else (half * (n // 2), n // 2)
        rows = pl.ds(pl.multiple_of(ln * n + first, 16), size)
        if s == 2:
            return WO.at[core, rows, :]
        return W.at[rows, pl.ds(512 * s, 512)]

    def over(s, yy, half, k, to, sem_s, sem_r):
        ref = part(s, yy, half)
        send(ref, ref, sem_s.at[s, k], sem_r, to)

    def to_x(s, yy, half, k):
        over(s, yy, half, k, x1 if half else x0, s_x, r_x.at[s, yy * 2 + half])

    def stage1(s):
        over(s, y, None, 0, up, s_y, r_y.at[s, 0])
        over(s, y, None, 1, down, s_y, r_y.at[s, 1])
        to_x(s, y, 0, 0)
        to_x(s, y, 1, 1)

    def stage2(s):
        got(part(s, ym, None), r_y.at[s, 0])
        over(s, ym, 0, 2, up, s_y, r_y.at[s, 2])
        to_x(s, ym, 0, 2)
        to_x(s, ym, 1, 3)
        got(part(s, yp, None), r_y.at[s, 1])
        over(s, yp, 1, 3, down, s_y, r_y.at[s, 3])
        to_x(s, yp, 0, 4)
        to_x(s, yp, 1, 5)

    def stage3(s):
        got(part(s, y2, 0), r_y.at[s, 2])
        to_x(s, y2, 0, 6)
        got(part(s, y2, 1), r_y.at[s, 3])
        to_x(s, y2, 1, 7)

    def stage4(s):
        for yy in range(4):
            for half in (0, 1):
                got(part(s, yy, half, 1 - xl), r_x.at[s, yy * 2 + half])

    def repack(Z, col):
        for j in range(16):
            FS[pl.ds(18 * j, 18), :] = Z[j].astype(F32)
        W[pl.ds(pl.multiple_of(line * LROWS, 16), LROWS), pl.ds(col, 512)] = FS[...].astype(BF)

    z_got(0, 1)
    local[1].wait()
    local[2].wait()
    repack(ZW, 0)
    stage1(0)
    z_got(2)
    local[3].wait()
    repack(ZQ, 512)

    @pl.loop(1, 16)
    def _(i):
        j = lax.rem(me + i, 16)
        got(SEGW.at[16 + j], r_s.at[j])

    local[5].wait()
    send(SEGW.at[pl.ds(16, 16)], SEGW.at[pl.ds(0, 16)], s_m.at[2], r_m.at[2], nxt8)
    for half in (0, 1):
        row = SEGW[16 + 2 * z + half].astype(F32)
        QS[pl.ds(half * TOK, TOK), :] = jnp.broadcast_to(row, (TOK, TOK)).T

    stage2(0)
    stage3(0)
    stage1(1)

    def project(col, xx, add):
        @pl.loop(0, 2)
        def _(i):
            rows = pl.ds(pl.multiple_of(i * TOK, TOK), TOK)
            w = W[pl.ds(pl.multiple_of(xx * (D // 2), 16), D // 2), pl.ds(col, 512)]
            term = jnp.dot(N[xx, rows, :], w, preferred_element_type=F32)
            ACC[rows, :] = ACC[rows, :] + term if add else term

    def turned(rows, col):
        a, b = ACC[rows, pl.ds(col, 128)], ACC[rows, pl.ds(col + 128, 128)]
        c, s = cos[rows, :], sin[rows, :]
        return (a * c - b * s).astype(BF), (b * c + a * s).astype(BF)

    project(0, xl, False)
    stage4(0)
    project(0, 1 - xl, True)
    for half, buf in ((1, B), (0, A)):
        rows = pl.ds(half * TOK, TOK)
        low, high = turned(rows, 0)
        buf[0, 0, :, pl.ds(0, 128)] = low
        buf[0, 0, :, pl.ds(128, 128)] = high
        buf[0, 1] = ACC[rows, pl.ds(256, 256)].astype(BF)

    for kv in (0, 1):
        send(B.at[0, kv], B.at[8, kv], s_b.at[0, kv], r_b.at[8, kv], nxt8)
    for kv in (0, 1):
        send(A.at[0, kv], A.at[1, kv], s_a.at[0, kv], r_a.at[1, kv], nxt)
    for kv in (0, 1):
        send(A.at[0, kv], A.at[8, kv], s_a.at[8, kv], r_a.at[8, kv], nxt8)

    got(SEGW.at[pl.ds(0, 16)], r_m.at[2])

    def pass_a(j, kv):
        return rc(A.at[j, kv], A.at[j + 1, kv], s_a.at[j, kv], r_a.at[j + 1, kv], nxt)

    def pass_b(t, kv):
        return rc(B.at[t, kv], B.at[t - 1, kv], s_b.at[t, kv], r_b.at[t - 1, kv], prv)

    def relay(j):
        t = 9 - j
        for kv in (0, 1):
            got(A.at[j, kv], r_a.at[j, kv])

            @pl.when(j <= 6)
            def _():
                pass_a(j, kv).start()

            got(B.at[t, kv], r_b.at[t, kv])

            @pl.when(j <= 7)
            def _():
                pass_b(t, kv).start()

    stage2(1)
    stage3(1)
    relay(1)
    project(512, xl, False)
    stage4(1)
    project(512, 1 - xl, True)
    for h in (0, 1):
        for half in (0, 1):
            rows = pl.ds(half * TOK, TOK)
            low, high = turned(rows, 256 * h)
            dst = pl.ds(h * CHIP + half * TOK, TOK)
            QQ[dst, pl.ds(0, 128)] = low
            QQ[dst, pl.ds(128, 128)] = high

    O[...] = jnp.zeros_like(O)
    L[...] = jnp.zeros_like(L)

    def attend(buf, t, half):
        index = 16 + 2 * z + half - 2 * t
        shut = jnp.logical_and(index < 16, line == 0)
        docs = jnp.where(shut, -1.0, SEGW[index].astype(F32))
        first = half * TOK - CHIP * t

        @pl.loop(0, 4)
        def _(r):
            rows = pl.ds(pl.multiple_of(r * TOK, TOK), TOK)
            tok = pl.multiple_of(lax.rem(r, 2) * TOK, TOK)
            s = lax.dot_general(
                QQ[rows, :], buf[t, 0], (((1,), (1,)), ((), ())), preferred_element_type=F32
            )
            w = jnp.exp2(jnp.tanh(s * (1.0 / (16.0 * CAP))) * (CAP * LOG2E))
            behind = (
                lax.broadcasted_iota(I32, (TOK, TOK), 0)
                - lax.broadcasted_iota(I32, (TOK, TOK), 1)
                + (tok - first)
            )
            allowed = (behind >= 0) & (behind < WINDOW) & (QS[pl.ds(tok, TOK), :] == docs)
            w = jnp.where(allowed, w, 0.0)
            L[rows, :] += w[:, :128] + w[:, 128:]
            O[rows, :] += jnp.dot(w.astype(BF), buf[t, 1], preferred_element_type=F32)

    z_got(3)
    local[4].wait()
    for j in range(0, 16, 2):
        pair = jnp.concatenate([ZO[j].astype(F32), ZO[j + 1].astype(F32)], axis=0)
        WO[core, pl.ds(pl.multiple_of(line * OROWS + 8 * j, 16), 16), :] = pair.astype(BF)
    stage1(2)

    attend(B, 0, 1)
    attend(A, 0, 0)
    attend(A, 1, 0)
    attend(B, 8, 1)

    def step(j):
        relay(j)
        attend(A, j, 0)
        attend(B, 9 - j, 1)

    step(2)
    stage2(2)
    step(3)
    stage3(2)
    step(4)
    step(5)
    stage4(2)
    send(WO.at[core], WO.at[core], s_m.at[3], r_m.at[3], mate)
    pl.loop(6, 9)(step)

    for g in (0, 1):
        @pl.when(core == g)
        def _():
            for h in (0, 1):
                for half in (0, 1):
                    rows = pl.ds(h * CHIP + half * TOK, TOK)
                    att = O[rows, :] / jnp.sum(L[rows, :], axis=-1, keepdims=True)
                    if half == g:
                        ATT[g, :, pl.ds(h * HEAD, HEAD)] = att.astype(BF)
                    else:
                        SB[:, pl.ds(h * HEAD, HEAD)] = att.astype(BF)

    send(SB, ATT.at[core], s_m.at[4], r_m.at[4], mate)
    got(WO.at[other], r_m.at[3])
    got(ATT.at[other], r_m.at[4])

    for c in (0, 1):
        cols = pl.ds(c * (D // 2), D // 2)
        BR[:, cols] = jnp.dot(ATT[0], WO[c, pl.ds(0, 512), :], preferred_element_type=F32) + jnp.dot(
            ATT[1], WO[c, pl.ds(512, 512), :], preferred_element_type=F32
        )

    @pl.loop(0, TOK // 32)
    def _(i):
        rows = pl.ds(pl.multiple_of(i * 32, 32), 32)
        v = BR[rows, :]
        v = v * lax.rsqrt(jnp.mean(v * v, axis=-1, keepdims=True) + EPS) * post[...]
        x = H[pl.ds(pl.multiple_of(core * TOK + i * 32, 32), 32), :].astype(F32)
        out[rows, :] = (x + v).astype(BF)

    for copy in sends:
        copy.wait_send()

    @pl.loop(1, 8)
    def _(j):
        for kv in (0, 1):
            @pl.when(j <= 6)
            def _():
                pass_a(j, kv).wait_send()

            pass_b(9 - j, kv).wait_send()

    @pl.loop(1, 8)
    def _(d):
        for c in (0, 1):
            seg_copy(2 * d + c, z_dev(d, c)).wait_send()
            for p in range(4):
                z_copies(p, 2 * d + c, c, z_dev(d, c)).wait_send()

    seg_copy(0, mate).wait_send()
    for p in range(4):
        z_copies(p, 0, other, mate).wait_send()


def per_device(hidden_in, segment_ids, pre_gain, w_qkv, w_out, post_gain):
    chip = lax.axis_index("seq") // 2
    positions = chip * CHIP + jnp.arange(CHIP, dtype=I32)
    inverse = 1.0 / 10000.0 ** (jnp.arange(HEAD // 2, dtype=F32) * 2.0 / HEAD)
    angles = positions.astype(F32)[:, None] * inverse[None, :]
    hbm = pl.BlockSpec(memory_space=pltpu.HBM)
    vmem = pl.BlockSpec(memory_space=pltpu.VMEM)
    dma = pltpu.SemaphoreType.DMA
    result = pl.pallas_call(
        kernel,
        out_shape=jax.ShapeDtypeStruct((TOK, D), BF),
        in_specs=[hbm] * 4 + [vmem] * 4,
        out_specs=vmem,
        scratch_shapes=[
            pltpu.VMEM((CHIP, D), BF),
            pltpu.VMEM((2, CHIP, D // 2), BF),
            pltpu.VMEM((D, 1024), BF),
            pltpu.VMEM((2, 1024, D // 2), BF),
            pltpu.VMEM((16, 18, 512), BF),
            pltpu.VMEM((16, 18, 512), BF),
            pltpu.VMEM((16, 8, D // 2), BF),
            pltpu.VMEM((LROWS, 512), F32),
            pltpu.VMEM((CHIP, 512), F32),
            pltpu.VMEM((2 * CHIP, HEAD), BF),
            pltpu.VMEM((2 * CHIP, HEAD), F32),
            pltpu.VMEM((2 * CHIP, 128), F32),
            pltpu.VMEM((9, 2, TOK, HEAD), BF),
            pltpu.VMEM((9, 2, TOK, HEAD), BF),
            pltpu.VMEM((32, 1, TOK), I32),
            pltpu.VMEM((CHIP, TOK), F32),
            pltpu.VMEM((2, TOK, 512), BF),
            pltpu.VMEM((TOK, 512), BF),
            pltpu.VMEM((TOK, D), F32),
            dma((6,)),
            dma((4, 16)), dma((4, 16)),
            dma((16,)), dma((16,)),
            dma((3, 4)), dma((3, 4)),
            dma((3, 8)), dma((3, 8)),
            dma((9, 2)), dma((9, 2)),
            dma((9, 2)), dma((9, 2)),
            dma((5,)), dma((5,)),
        ],
        compiler_params=pltpu.CompilerParams(
            collective_id=0, has_side_effects=True, vmem_limit_bytes=60 * 1024 * 1024
        ),
    )(
        hidden_in[0],
        segment_ids,
        w_qkv,
        w_out,
        jnp.cos(angles),
        jnp.sin(angles),
        pre_gain.reshape(1, D),
        post_gain.reshape(1, D),
    )
    return result[None]


def solution(mesh):
    placed = (P("batch", "seq", None), P("batch", "seq"), P(), P("seq", None), P("seq", None), P())
    return jax.shard_map(
        per_device, mesh=mesh, in_specs=placed, out_specs=P("batch", "seq", None), check_vma=False
    )
```

time: 529 us -> 158 us (0.30)
  the two profiles are of different devices: /device:TPU:6 before, /device:TPU:11 now
where the time goes in v1:
time: 158 us
  Pallas kernels  151 us (96%)
  local copies, waits for them, and re-layouts  4.98 us (3%)
  other arithmetic  1.81 us (1%)
    pallas_call x1, Pallas kernels, per_device(): pl.pallas_call(kernel, out_shape=jax.ShapeDtypeStruct((TOK, D), BF), in_s...  151 us

profile of v1, /device:TPU:11, one launch (start us, length us, event | category | flops | bytes accessed | tf_op | source)
XLA Modules:
  0.0 157.8 jit_solution(6864061878347833569)
XLA Ops:
  0.0 1.3 reshape.17.pre
  1.3 1.3 reshape.18.post
  2.6 1.8 %multiply_sine_fusion = (f32[512,128]{1,0:T(8,128)}, f32[512,128]{1,0:T(8,128)}) fusion(f32[128]{0:T(128)S(1)} %negate_power_fusion, f32[512]{0:T(512)S(1)} %add_convert_fusion), kind=kLoop, calls=%fused_computation | loop fusion | flops 65536 | bytes 526848 | tf_op jit(solution)/shard_map/sin | solution.py:474
  4.4 151.0 %shard_map.64 = bf16[256,2304]{1,0:T(8,128)(2,1)} custom-call(bf16[256,2304]{1,0:T(8,128)(2,1)} %bitcast.3, s32[1,256]{1,0:T(1,128)} %seg.1, bf16[18,2048]{1,0:T(8,128)(2,1)} %wqkv.1, bf16[8,2304]{1,0:T(8,128)(2,1)} %wout.1, f32[512,128]{1,0:T(8,128)} %get-tuple-element.6.cos, f32[512,128]{1,0:T(8,128)} %get-tuple-element.5.sin, f32[1,2304]{1,0:T(1,128)} %reshape.17.pre, ...), custom_call_target="tpu_custom_call" | custom-call | tf_op jit(solution)/shard_map/pallas_call | solution.py:431
  155.4 2.4 %copy.8 = bf16[1,256,2304]{2,1,0:T(8,128)(2,1)} copy(bf16[1,256,2304]{2,1,0:T(8,128)(2,1)} %bitcast.2) | data formatting | bytes 2359296
  (2 shorter events, 0.0 us)

commit v2 on v1

v2 whole, which is shorter than its diff:
```python
import jax
import jax.numpy as jnp
from jax import lax
from jax.experimental import pallas as pl
from jax.experimental.pallas import tpu as pltpu
from jax.sharding import PartitionSpec as P

MESH = pl.DeviceIdType.MESH
BF, F32, I32 = jnp.bfloat16, jnp.float32, jnp.int32

D = 2304
HEAD = 256
WINDOW = 4096
TOK = 256
CHIP = 512
SEQ_DEV = 128
LINES = 8
LROWS = 288
OROWS = 128
LAG = 3
EPS = 1e-06
CAP = 50.0
LOG2E = 1.4426950408889634


def kernel(
    hid, seg, wqkv, wout, inverse, pre18, post18, out,
    cos, sin, pre, post, H, N, W, WO, ZW, ZQ, ZO, FS, ACC, QQ, O, L, A, B, RA, RB, SEGW, QS, ATT, SB, BR,
    s_loc, s_z, r_z, s_y, r_y, s_x, r_x, s_a, r_a, s_b, r_b, s_d, r_d, s_m, r_m,
):
    seq = lax.axis_index("seq")
    bat = lax.axis_index("batch")
    core = lax.rem(seq, 2)
    other = 1 - core
    me = lax.rem(seq, 16)
    z = lax.div(me, 2)
    line = lax.div(seq, 16)
    y = lax.rem(line, 4)
    xl = lax.div(line, 4)

    def dev(s, b=bat):
        return {"seq": s, "batch": b}

    def at_line(xx, yy):
        return (xx * 4 + yy) * 16 + me

    yp, ym, y2 = lax.rem(y + 1, 4), lax.rem(y + 3, 4), lax.rem(y + 2, 4)
    up, down = dev(at_line(xl, yp)), dev(at_line(xl, ym))
    x0, x1 = dev(at_line(1 - xl, y)), dev(at_line(1 - xl, y), 1 - bat)
    nxt, prv = dev(lax.rem(seq + 2, SEQ_DEV)), dev(lax.rem(seq + 126, SEQ_DEV))
    nxt8, prv8 = dev(lax.rem(seq + 16, SEQ_DEV)), dev(lax.rem(seq + 112, SEQ_DEV))
    mate = dev(seq + 1 - 2 * core)
    z0, z7 = dev(line * 16 + core), dev(line * 16 + 14 + core)

    def z_dev(d, c):
        return dev(line * 16 + lax.rem(z + d, 8) * 2 + c)

    def rc(src, dst, ss, rs, to):
        return pltpu.make_async_remote_copy(
            src_ref=src, dst_ref=dst, send_sem=ss, recv_sem=rs, device_id=to, device_id_type=MESH
        )

    def got(ref, rs):
        rc(ref, ref, s_m.at[0], rs, mate).wait_recv()

    def gone(ref, ss):
        rc(ref, ref, ss, r_m.at[0], mate).wait_send()

    sends = []

    def send(src, dst, ss, rs, to):
        copy = rc(src, dst, ss, rs, to)
        copy.start()
        sends.append(copy)

    barrier = pltpu.get_barrier_semaphore()

    def greet(to):
        pl.semaphore_signal(barrier, inc=1, device_id=to, device_id_type=MESH)

    @pl.loop(1, 8)
    def _(d):
        greet(z_dev(d, 0))
        greet(z_dev(d, 1))

    for to in (mate, up, down, x0, x1, nxt, prv, nxt8, prv8):
        greet(to)

    own = pl.ds(pl.multiple_of(core * TOK, TOK), TOK)
    local = [
        pltpu.make_async_copy(hid, H.at[own], s_loc.at[0]),
        pltpu.make_async_copy(
            wqkv.at[:, pl.ds(pl.multiple_of(1024 + 256 * core, 256), 256)],
            ZW.at[me, :, pl.ds(0, 256)],
            s_loc.at[1],
        ),
        pltpu.make_async_copy(
            wqkv.at[:, pl.ds(pl.multiple_of(1536 + 256 * core, 256), 256)],
            ZW.at[me, :, pl.ds(256, 256)],
            s_loc.at[2],
        ),
        pltpu.make_async_copy(
            wqkv.at[:, pl.ds(pl.multiple_of(512 * core, 512), 512)], ZQ.at[me], s_loc.at[3]
        ),
        pltpu.make_async_copy(
            wout.at[:, pl.ds(pl.multiple_of(1152 * core, 128), 1152)], ZO.at[me], s_loc.at[4]
        ),
        pltpu.make_async_copy(seg, SEGW.at[16 + me], s_loc.at[5]),
    ]
    for copy in local:
        copy.start()

    pl.semaphore_wait(barrier, 23)

    def z_copies(p, c, to):
        if p == 0:
            src, dst = wqkv.at[:, pl.ds(pl.multiple_of(1024 + 256 * c, 256), 256)], ZW.at[me, :, pl.ds(0, 256)]
        elif p == 1:
            src, dst = wqkv.at[:, pl.ds(pl.multiple_of(1536 + 256 * c, 256), 256)], ZW.at[me, :, pl.ds(256, 256)]
        elif p == 2:
            src, dst = wqkv.at[:, pl.ds(pl.multiple_of(512 * c, 512), 512)], ZQ.at[me]
        else:
            src, dst = wout.at[:, pl.ds(pl.multiple_of(1152 * c, 128), 1152)], ZO.at[me]
        return rc(src, dst, s_z.at[p], r_z.at[p], to)

    def z_send(*pieces):
        @pl.loop(1, 8)
        def _(d):
            for c in (0, 1):
                for p in pieces:
                    z_copies(p, c, z_dev(d, c)).start()

        for p in pieces:
            z_copies(p, other, mate).start()

    def z_others(p):
        if p == 0:
            return ZW.at[pl.ds(0, 15), :, pl.ds(0, 256)]
        if p == 1:
            return ZW.at[pl.ds(0, 15), :, pl.ds(256, 256)]
        return ZQ.at[pl.ds(0, 15)] if p == 2 else ZO.at[pl.ds(0, 15)]

    def z_got(*pieces):
        for p in pieces:
            got(z_others(p), r_z.at[p])

    def seg_copy(to):
        return rc(seg, SEGW.at[16 + me], s_m.at[5], r_m.at[5], to)

    z_send(0, 1)
    send(hid, H.at[own], s_m.at[1], r_m.at[1], mate)

    @pl.loop(1, 8)
    def _(d):
        for c in (0, 1):
            seg_copy(z_dev(d, c)).start()

    seg_copy(mate).start()

    def norm_rows(first):
        @pl.loop(0, TOK // 64)
        def _(i):
            rows = pl.ds(pl.multiple_of(first + i * 64, 64), 64)
            v = H[rows, :].astype(F32)
            v = v * lax.rsqrt(jnp.mean(v * v, axis=-1, keepdims=True) + EPS) * pre[...]
            v = v.astype(BF)
            N[0, rows, :] = v[:, : D // 2]
            N[1, rows, :] = v[:, D // 2 :]

    for i in range(D // 128):
        pre[:, pl.ds(128 * i, 128)] = pre18[pl.ds(i, 1), :]
        post[:, pl.ds(128 * i, 128)] = post18[pl.ds(i, 1), :]
    local[0].wait()
    norm_rows(core * TOK)
    theirs = pl.ds(pl.multiple_of(other * TOK, TOK), TOK)
    got(H.at[theirs], r_m.at[1])
    norm_rows(other * TOK)

    @pl.loop(0, CHIP // 64)
    def _(i):
        rows = pl.ds(pl.multiple_of(i * 64, 64), 64)
        places = lax.div(seq, 2) * CHIP + i * 64 + lax.broadcasted_iota(I32, (64, HEAD // 2), 0)
        angles = places.astype(F32) * inverse[...]
        cos[rows, :] = jnp.cos(angles)
        sin[rows, :] = jnp.sin(angles)

    def part(s, yy, half, xx=xl):
        ln = xx * 4 + yy
        n = OROWS if s == 2 else LROWS
        first, size = (0, n) if half is None else (half * (n // 2), n // 2)
        rows = pl.ds(pl.multiple_of(ln * n + first, 16), size)
        if s == 2:
            return WO.at[core, rows, :]
        return W.at[rows, pl.ds(512 * s, 512)]

    def to_y(s, yy, half, to, k):
        ref = part(s, yy, half)
        rc(ref, ref, s_y.at[s], r_y.at[s, k], to).start()

    def to_x(s, yy, half):
        ref = part(s, yy, half)
        rc(ref, ref, s_x.at[s], r_x.at[s], x1 if half else x0).start()

    def stage1_up(s):
        to_y(s, y, 0, up, 0)
        to_y(s, y, 1, up, 1)

    def stage1(s):
        to_y(s, y, 1, down, 3)
        to_y(s, y, 0, down, 2)
        to_x(s, y, 0)
        to_x(s, y, 1)

    def from_below(s, half):
        got(part(s, ym, half), r_y.at[s, half])
        if s == 0 and half == 0:
            to_y(s, ym, 0, up, 4)
        to_x(s, ym, half)

    def from_above(s, half):
        got(part(s, yp, half), r_y.at[s, 2 + half])
        if s > 0 or half == 1:
            to_y(s, yp, half, down, 4 + half)
        to_x(s, yp, half)

    def stage2_up(s):
        from_below(s, 0)
        from_below(s, 1)

    def stage2(s):
        from_above(s, 1)
        from_above(s, 0)

    def from_second(s, half):
        got(part(s, y2, half), r_y.at[s, 4 + half])
        to_x(s, y2, half)

    def stage3(s):
        from_second(s, 0)
        from_second(s, 1)

    def stage4(s):
        n = 4 * (OROWS if s == 2 else LROWS)
        first = pl.multiple_of((1 - xl) * n, 16)
        if s == 2:
            got(WO.at[core, pl.ds(first, n), :], r_x.at[s])
        else:
            got(W.at[pl.ds(first, n), pl.ds(512 * s, 512)], r_x.at[s])

    def streams_gone(s):
        n = OROWS if s == 2 else LROWS
        for rows, sem in ((3 * n, s_y.at[s]), (4 * n, s_x.at[s])):
            if s == 2:
                gone(WO.at[core, pl.ds(0, rows), :], sem)
            else:
                gone(W.at[pl.ds(0, rows), pl.ds(512 * s, 512)], sem)

    def repack(Z, col):
        for j in range(16):
            FS[pl.ds(18 * j, 18), :] = Z[j].astype(F32)
        W[pl.ds(pl.multiple_of(line * LROWS, 16), LROWS), pl.ds(col, 512)] = FS[...].astype(BF)

    z_got(0, 1)
    local[1].wait()
    local[2].wait()
    repack(ZW, 0)
    stage1_up(0)
    stage1(0)
    z_send(2)
    from_below(0, 0)
    from_above(0, 1)
    from_below(0, 1)
    from_above(0, 0)
    z_send(3)
    stage3(0)
    z_got(2)
    local[3].wait()
    repack(ZQ, 512)
    stage1_up(1)
    stage1(1)

    def project(col, xx, add):
        @pl.loop(0, 2)
        def _(i):
            rows = pl.ds(pl.multiple_of(i * TOK, TOK), TOK)
            w = W[pl.ds(pl.multiple_of(xx * (D // 2), 16), D // 2), pl.ds(col, 512)]
            term = jnp.dot(N[xx, rows, :], w, preferred_element_type=F32)
            ACC[rows, :] = ACC[rows, :] + term if add else term

    def turned(rows, col):
        a, b = ACC[rows, pl.ds(col, 128)], ACC[rows, pl.ds(col + 128, 128)]
        c, s = cos[rows, :], sin[rows, :]
        return (a * c - b * s).astype(BF), (b * c + a * s).astype(BF)

    project(0, xl, False)

    got(SEGW.at[pl.ds(16, 15)], r_m.at[5])
    local[5].wait()
    send(SEGW.at[pl.ds(16, 16)], SEGW.at[pl.ds(0, 16)], s_m.at[2], r_m.at[2], nxt8)
    for half in (0, 1):
        row = SEGW[16 + 2 * z + half].astype(F32)
        QS[pl.ds(half * TOK, TOK), :] = jnp.broadcast_to(row, (TOK, TOK)).T

    stage4(0)
    project(0, 1 - xl, True)
    for half, buf in ((1, B), (0, A)):
        rows = pl.ds(half * TOK, TOK)
        low, high = turned(rows, 0)
        buf[0, 0, :, pl.ds(0, 128)] = low
        buf[0, 0, :, pl.ds(128, 128)] = high
        buf[0, 1] = ACC[rows, pl.ds(256, 256)].astype(BF)

    def piece(buf, t, c):
        return buf.at[t, c // 2, pl.ds(c % 2 * 128, 128), :]

    def stop(buf, k, c):
        return buf.at[k, pl.ds(c % 2 * 128, 128), :]

    def pass_on(buf, t, u, c, ss, rs, to):
        rc(piece(buf, t, c), piece(buf, u, c), ss, rs.at[u, c], to).start()

    def pass_a(j, c):
        @pl.when(z != 7)
        def _():
            pass_on(A, j, j + 1, c, s_a.at[0], r_a, nxt)

        @pl.when(z == 7)
        def _():
            to = nxt8 if c < 2 else z0
            rc(piece(A, j, c), stop(RA, j, c), s_a.at[0], r_d.at[0, j, c % 2], to).start()

    def pass_b(j, c):
        t = 9 - j

        @pl.when(z != 0)
        def _():
            pass_on(B, t, t - 1, c, s_b.at[0], r_b, prv)

        @pl.when(z == 0)
        def _():
            to = z7 if c < 2 else prv8
            rc(piece(B, t, c), stop(RB, j - 1, c), s_b.at[0], r_d.at[1, j - 1, c % 2], to).start()

    def take_a(e):
        j, c = divmod(e, 4)
        if 1 <= j <= 8:
            got(piece(A, j, c), r_a.at[j, c])
        if 1 <= j <= 6:
            pass_a(j, c)

    def take_b(e):
        j, c = divmod(e, 4)
        if 1 <= j <= 8:
            got(piece(B, 9 - j, c), r_b.at[9 - j, c])
        if 1 <= j <= 7:
            pass_b(j, c)

    def help_on(e, here):
        j, c = divmod(e, 4)
        if here != (7 if c < 2 else 0):
            return
        if 0 <= j <= 6:
            ref = stop(RA, j, c)
            got(ref, r_d.at[0, j, c % 2])
            to = z0 if c < 2 else nxt8
            rc(ref, piece(A, j + 1, c), s_d.at[0], r_a.at[j + 1, c], to).start()
        if 1 <= j <= 7:
            ref = stop(RB, j - 1, c)
            got(ref, r_d.at[1, j - 1, c % 2])
            to = prv8 if c < 2 else z7
            rc(ref, piece(B, 8 - j, c), s_d.at[0], r_b.at[8 - j, c], to).start()

    def relay(e):
        @pl.when(z == 0)
        def _():
            take_b(e)
            help_on(e - LAG, 0)
            take_a(e - LAG)

        @pl.when(z == 7)
        def _():
            take_a(e)
            help_on(e - LAG, 7)
            take_b(e - LAG)

        @pl.when((z > 0) & (z < 4))
        def _():
            take_b(e)
            take_a(e)

        @pl.when((z > 3) & (z < 7))
        def _():
            take_a(e)
            take_b(e)

    for c in range(4):
        pass_on(B, 0, 8, c, s_b.at[1], r_b, nxt8)
        pass_a(0, c)

    def attend(j, part):
        blocks = ((A, 0, 0), (B, 0, 1)) if j == 0 else ((A, j, 0), (B, 9 - j, 1))
        docs, firsts = [], []
        for _, t, half in blocks:
            index = 16 + 2 * z + half - 2 * t
            shut = jnp.logical_and(index < 16, line == 0)
            docs.append(jnp.where(shut, -1.0, SEGW[index].astype(F32)))
            firsts.append(half * TOK - CHIP * t)

        @pl.loop(2 * part, 2 * part + 2, unroll=2)
        def _(r):
            rows = pl.ds(pl.multiple_of(r * TOK, TOK), TOK)
            tok = pl.multiple_of(lax.rem(r, 2) * TOK, TOK)
            queries, whose = QQ[rows, :], QS[pl.ds(tok, TOK), :]
            sums, mixed = None, None
            for (buf, t, _), doc, first in zip(blocks, docs, firsts):
                s = lax.dot_general(
                    queries, buf[t, 0], (((1,), (1,)), ((), ())), preferred_element_type=F32
                )
                w = jnp.exp2(jnp.tanh(s * (1.0 / (16.0 * CAP))) * (CAP * LOG2E))
                allowed = whose == doc
                if t in (0, 8):
                    behind = (
                        lax.broadcasted_iota(I32, (TOK, TOK), 0)
                        - lax.broadcasted_iota(I32, (TOK, TOK), 1)
                        + (tok - first)
                    )
                    allowed &= (behind >= 0) & (behind < WINDOW)
                w = jnp.where(allowed, w, 0.0)
                part_sum = w[:, :128] + w[:, 128:]
                term = jnp.dot(w.astype(BF), buf[t, 1], preferred_element_type=F32)
                sums = part_sum if sums is None else sums + part_sum
                mixed = term if mixed is None else mixed + term
            if j == 0:
                L[rows, :] = sums
                O[rows, :] = mixed
            else:
                L[rows, :] += sums
                O[rows, :] += mixed

    def relays(first, last):
        for e in range(first, last):
            relay(e)
            for action in extra.get(e, ()):
                action()

    eighth = [lambda c=c: pass_on(A, 0, 8, c, s_a.at[1], r_a, nxt8) for c in range(4)]
    extra = {
        11: [lambda: to_y(2, y, 0, up, 0)],
        12: [lambda: to_y(2, y, 1, down, 3)],
        14: [lambda: to_y(2, y, 1, up, 1)],
        16: [lambda: to_y(2, y, 0, down, 2), lambda: to_x(2, y, 0), lambda: to_x(2, y, 1)],
        17: [eighth[0]],
        18: [lambda: from_above(2, 1)],
        19: [eighth[1]],
        20: [lambda: from_below(2, 0)],
        21: [eighth[2]],
        22: [lambda: from_above(2, 0)],
        23: [eighth[3]],
        24: [lambda: from_below(2, 1)],
        27: [lambda: from_second(2, 1)],
        29: [lambda: from_second(2, 0)],
        33: [
            lambda: stage4(2),
            lambda: send(WO.at[core], WO.at[core], s_m.at[3], r_m.at[3], mate),
        ],
    }

    relays(LAG, 8)
    stage2(1)

    z_got(3)
    local[4].wait()
    for j in range(0, 16, 2):
        pair = jnp.concatenate([ZO[j].astype(F32), ZO[j + 1].astype(F32)], axis=0)
        WO[core, pl.ds(pl.multiple_of(line * OROWS + 8 * j, 16), 16), :] = pair.astype(BF)

    gone(SEGW.at[pl.ds(0, 15)], s_m.at[5])
    for p in range(4):
        gone(z_others(p), s_z.at[p])

    relays(8, 12)
    stage2_up(1)
    stage3(1)
    relays(12, 14)
    project(512, xl, False)
    relays(14, 16)
    stage4(1)
    project(512, 1 - xl, True)
    for h in (0, 1):
        for half in (0, 1):
            rows = pl.ds(half * TOK, TOK)
            low, high = turned(rows, 256 * h)
            dst = pl.ds(h * CHIP + half * TOK, TOK)
            QQ[dst, pl.ds(0, 128)] = low
            QQ[dst, pl.ds(128, 128)] = high
    got(SEGW.at[pl.ds(0, 16)], r_m.at[2])

    todo = [(j, p) for j in range(9) for p in (0, 1)]
    for e in range(16, 36 + LAG):
        relays(e, e + 1)
        if todo and 4 * todo[0][0] + 3 + LAG <= e:
            attend(*todo.pop(0))
    for j, p in todo:
        attend(j, p)

    def attended(half, put):
        for h in (0, 1):
            rows = pl.ds(pl.multiple_of(h * CHIP + half * TOK, TOK), TOK)
            share = 1.0 / jnp.sum(L[rows, :], axis=-1, keepdims=True)
            put(h, (O[rows, :] * share).astype(BF))

    def put_other(h, value):
        SB[:, pl.ds(h * HEAD, HEAD)] = value

    def put_own(h, value):
        ATT[core, :, pl.ds(h * HEAD, HEAD)] = value

    attended(other, put_other)
    send(SB, ATT.at[core], s_m.at[4], r_m.at[4], mate)
    attended(core, put_own)
    got(WO.at[other], r_m.at[3])

    def branch(g, add):
        for c in (0, 1):
            cols = pl.ds(c * (D // 2), D // 2)
            weights = WO[c, pl.ds(pl.multiple_of(g * 512, 512), 512), :]
            term = jnp.dot(ATT[g], weights, preferred_element_type=F32)
            BR[:, cols] = BR[:, cols] + term if add else term

    branch(core, False)
    got(ATT.at[other], r_m.at[4])
    branch(other, True)

    @pl.loop(0, TOK // 32)
    def _(i):
        rows = pl.ds(pl.multiple_of(i * 32, 32), 32)
        v = BR[rows, :]
        v = v * lax.rsqrt(jnp.mean(v * v, axis=-1, keepdims=True) + EPS) * post[...]
        x = H[pl.ds(pl.multiple_of(core * TOK + i * 32, 32), 32), :].astype(F32)
        out[rows, :] = (x + v).astype(BF)

    for copy in sends:
        copy.wait_send()
    for buf, sem in ((A, s_a), (B, s_b)):
        gone(buf.at[pl.ds(0, 7)], sem.at[0])
        gone(buf.at[0], sem.at[1])
    @pl.when(lax.rem(z, 7) == 0)
    def _():
        gone(A.at[pl.ds(0, 7)], s_d.at[0])

    for stream in range(3):
        streams_gone(stream)


def per_device(hidden_in, segment_ids, pre_gain, w_qkv, w_out, post_gain):
    inverse = 1.0 / 10000.0 ** (jnp.arange(HEAD // 2, dtype=F32) * 2.0 / HEAD)
    hbm = pl.BlockSpec(memory_space=pltpu.HBM)
    vmem = pl.BlockSpec(memory_space=pltpu.VMEM)
    dma = pltpu.SemaphoreType.DMA
    result = pl.pallas_call(
        kernel,
        out_shape=pltpu.VMEM((TOK, D), BF),
        in_specs=[hbm] * 4 + [vmem] * 3,
        out_specs=vmem,
        scratch_shapes=[
            pltpu.VMEM((CHIP, HEAD // 2), F32),
            pltpu.VMEM((CHIP, HEAD // 2), F32),
            pltpu.VMEM((1, D), F32),
            pltpu.VMEM((1, D), F32),
            pltpu.VMEM((CHIP, D), BF),
            pltpu.VMEM((2, CHIP, D // 2), BF),
            pltpu.VMEM((D, 1024), BF),
            pltpu.VMEM((2, 1024, D // 2), BF),
            pltpu.VMEM((16, 18, 512), BF),
            pltpu.VMEM((16, 18, 512), BF),
            pltpu.VMEM((16, 8, D // 2), BF),
            pltpu.VMEM((LROWS, 512), F32),
            pltpu.VMEM((CHIP, 512), F32),
            pltpu.VMEM((2 * CHIP, HEAD), BF),
            pltpu.VMEM((2 * CHIP, HEAD), F32),
            pltpu.VMEM((2 * CHIP, 128), F32),
            pltpu.VMEM((9, 2, TOK, HEAD), BF),
            pltpu.VMEM((9, 2, TOK, HEAD), BF),
            pltpu.VMEM((7, TOK, HEAD), BF),
            pltpu.VMEM((7, TOK, HEAD), BF),
            pltpu.VMEM((32, 1, TOK), I32),
            pltpu.VMEM((CHIP, TOK), F32),
            pltpu.VMEM((2, TOK, 512), BF),
            pltpu.VMEM((TOK, 512), BF),
            pltpu.VMEM((TOK, D), F32),
            dma((6,)),
            dma((4,)), dma((4,)),
            dma((3,)), dma((3, 6)),
            dma((3,)), dma((3,)),
            dma((2,)), dma((9, 4)),
            dma((2,)), dma((9, 4)),
            dma((1,)), dma((2, 7, 2)),
            dma((6,)), dma((6,)),
        ],
        compiler_params=pltpu.CompilerParams(
            collective_id=0, has_side_effects=True, vmem_limit_bytes=60 * 1024 * 1024
        ),
    )(
        hidden_in[0],
        segment_ids,
        w_qkv,
        w_out,
        inverse.reshape(1, HEAD // 2),
        pre_gain.reshape(D // 128, 128),
        post_gain.reshape(D // 128, 128),
    )
    return result[None]


def solution(mesh):
    placed = (P("batch", "seq", None), P("batch", "seq"), P(), P("seq", None), P("seq", None), P())
    return jax.shard_map(
        per_device, mesh=mesh, in_specs=placed, out_specs=P("batch", "seq", None), check_vma=False
    )
```

time: 158 us -> 114 us (0.72)
  the two profiles are of different devices: /device:TPU:11 before, /device:TPU:1 now
where the time goes in v2:
time: 114 us; the launch traced here: 113 us
  Pallas kernels  112 us (98%)
    pallas_call x1, Pallas kernels, per_device(): pl.pallas_call(kernel, out_shape=pltpu.VMEM((TOK, D), BF), in_specs=[hbm]...  112 us

profile of v2, /device:TPU:1, one launch (start us, length us, event | category | flops | bytes accessed | tf_op | source)
XLA Modules:
  0.0 113.4 jit_solution(6618864818747017730)
XLA Ops:
  0.0 0.5 negate_power_fusion.inverse
  0.5 111.8 %shard_map.64 = bf16[256,2304]{1,0:T(8,128)(2,1)S(1)} custom-call(bf16[256,2304]{1,0:T(8,128)(2,1)} %bitcast.5, s32[1,256]{1,0:T(1,128)} %seg.1, bf16[18,2048]{1,0:T(8,128)(2,1)} %wqkv.1, bf16[8,2304]{1,0:T(8,128)(2,1)} %wout.1, f32[1,128]{1,0:T(1,128)} %negate_power_fusion.inverse, f32[18,128]{1,0:T(8,128)} %bitcast.6, f32[18,128]{1,0:T(8,128)} %bitcast.7), custom_call_target="tpu_custom_call" | custom-call | tf_op jit(solution)/shard_map/pallas_call | solution.py:560
  112.4 1.0 copy.8

commit v3 on v2

--- a/solution.py
+++ b/solution.py
@@ -1,5 +1,6 @@
 import jax
 import jax.numpy as jnp
+import numpy as np
 from jax import lax
 from jax.experimental import pallas as pl
 from jax.experimental.pallas import tpu as pltpu
@@ -17,7 +18,9 @@
 LINES = 8
 LROWS = 288
 OROWS = 128
-LAG = 3
+LAGS = (2, 4, 3)
+LAG = max(LAGS)
+Q_AT = 19
 EPS = 1e-06
 CAP = 50.0
 LOG2E = 1.4426950408889634
@@ -26,7 +29,7 @@
 def kernel(
     hid, seg, wqkv, wout, inverse, pre18, post18, out,
     cos, sin, pre, post, H, N, W, WO, ZW, ZQ, ZO, FS, ACC, QQ, O, L, A, B, RA, RB, SEGW, QS, ATT, SB, BR,
-    s_loc, s_z, r_z, s_y, r_y, s_x, r_x, s_a, r_a, s_b, r_b, s_d, r_d, s_m, r_m,
+    s_loc, s_z, r_z, s_f, r_f, s_y, r_y, s_x, r_x, s_a, r_a, s_b, r_b, s_d, r_d, s_m, r_m,
 ):
     seq = lax.axis_index("seq")
     bat = lax.axis_index("batch")
@@ -124,8 +127,7 @@
         return rc(src, dst, s_z.at[p], r_z.at[p], to)
 
     def z_send(*pieces):
-        @pl.loop(1, 8)
-        def _(d):
+        for d in (1, 7, 2, 6):
             for c in (0, 1):
                 for p in pieces:
                     z_copies(p, c, z_dev(d, c)).start()
@@ -133,16 +135,35 @@
         for p in pieces:
             z_copies(p, other, mate).start()
 
-    def z_others(p):
+    def z_near(p):
         if p == 0:
-            return ZW.at[pl.ds(0, 15), :, pl.ds(0, 256)]
+            return ZW.at[pl.ds(0, 9), :, pl.ds(0, 256)]
         if p == 1:
-            return ZW.at[pl.ds(0, 15), :, pl.ds(256, 256)]
-        return ZQ.at[pl.ds(0, 15)] if p == 2 else ZO.at[pl.ds(0, 15)]
+            return ZW.at[pl.ds(0, 9), :, pl.ds(256, 256)]
+        return ZQ.at[pl.ds(0, 9)] if p == 2 else ZO.at[pl.ds(0, 9)]
 
     def z_got(*pieces):
         for p in pieces:
-            got(z_others(p), r_z.at[p])
+            got(z_near(p), r_z.at[p])
+
+    def z_forward(k):
+        Z = (ZW, ZQ, ZO)[k]
+
+        def on(d, to, cols=None):
+            slots = pl.ds(lax.rem(z + d, 8) * 2, 2)
+            ref = Z.at[slots] if cols is None else Z.at[slots, :, cols]
+            rc(ref, ref, s_f.at[k], r_f.at[k], z_dev(to, core)).start()
+
+        on(1, 6)
+        on(7, 2)
+        if k == 2:
+            on(2, 6)
+        else:
+            on(2, 6, pl.ds(0, 256))
+            on(6, 2, pl.ds(256, 256))
+
+    def z_far(k):
+        return (ZW, ZQ, ZO)[k].at[pl.ds(0, 6)]
 
     def seg_copy(to):
         return rc(seg, SEGW.at[16 + me], s_m.at[5], r_m.at[5], to)
@@ -197,9 +218,21 @@
         ref = part(s, yy, half)
         rc(ref, ref, s_y.at[s], r_y.at[s, k], to).start()
 
+    meet = jnp.where((lax.rem(y, 3) == 0) & (lax.rem(z, 7) == 0), 1, 0)
+    x0_out = dev(at_line(1 - xl, y), bat + meet * (1 - 2 * bat))
+
     def to_x(s, yy, half):
         ref = part(s, yy, half)
-        rc(ref, ref, s_x.at[s], r_x.at[s], x1 if half else x0).start()
+        if s < 2:
+            rc(ref, ref, s_x.at[s], r_x.at[s], x1 if half else x0).start()
+        else:
+            rc(ref, ref, s_x.at[s], r_x.at[2 + yy], x1 if half else x0_out).start()
+            rc(ref, ref, s_m.at[3], r_m.at[3], mate).start()
+
+    def across(yy):
+        ref = part(2, yy, None, 1 - xl)
+        got(ref, r_x.at[2 + yy])
+        rc(ref, ref, s_m.at[3], r_m.at[3], mate).start()
 
     def stage1_up(s):
         to_y(s, y, 0, up, 0)
@@ -240,12 +273,8 @@
         from_second(s, 1)
 
     def stage4(s):
-        n = 4 * (OROWS if s == 2 else LROWS)
-        first = pl.multiple_of((1 - xl) * n, 16)
-        if s == 2:
-            got(WO.at[core, pl.ds(first, n), :], r_x.at[s])
-        else:
-            got(W.at[pl.ds(first, n), pl.ds(512 * s, 512)], r_x.at[s])
+        first = pl.multiple_of((1 - xl) * (D // 2), 16)
+        got(W.at[pl.ds(first, D // 2), pl.ds(512 * s, 512)], r_x.at[s])
 
     def streams_gone(s):
         n = OROWS if s == 2 else LROWS
@@ -261,6 +290,8 @@
         W[pl.ds(pl.multiple_of(line * LROWS, 16), LROWS), pl.ds(col, 512)] = FS[...].astype(BF)
 
     z_got(0, 1)
+    z_forward(0)
+    got(z_far(0), r_f.at[0])
     local[1].wait()
     local[2].wait()
     repack(ZW, 0)
@@ -269,23 +300,27 @@
     z_send(2)
     from_below(0, 0)
     from_above(0, 1)
+    z_got(2)
+    z_forward(1)
     from_below(0, 1)
     from_above(0, 0)
     z_send(3)
     stage3(0)
-    z_got(2)
+    got(z_far(1), r_f.at[1])
     local[3].wait()
     repack(ZQ, 512)
     stage1_up(1)
     stage1(1)
 
+    def project_half(col, xx, add, i):
+        rows = pl.ds(i * TOK, TOK)
+        w = W[pl.ds(pl.multiple_of(xx * (D // 2), 16), D // 2), pl.ds(col, 512)]
+        term = jnp.dot(N[xx, rows, :], w, preferred_element_type=F32)
+        ACC[rows, :] = ACC[rows, :] + term if add else term
+
     def project(col, xx, add):
-        @pl.loop(0, 2)
-        def _(i):
-            rows = pl.ds(pl.multiple_of(i * TOK, TOK), TOK)
-            w = W[pl.ds(pl.multiple_of(xx * (D // 2), 16), D // 2), pl.ds(col, 512)]
-            term = jnp.dot(N[xx, rows, :], w, preferred_element_type=F32)
-            ACC[rows, :] = ACC[rows, :] + term if add else term
+        for i in (0, 1):
+            project_half(col, xx, add, i)
 
     def turned(rows, col):
         a, b = ACC[rows, pl.ds(col, 128)], ACC[rows, pl.ds(col + 128, 128)]
@@ -301,6 +336,8 @@
         row = SEGW[16 + 2 * z + half].astype(F32)
         QS[pl.ds(half * TOK, TOK), :] = jnp.broadcast_to(row, (TOK, TOK)).T
 
+    z_got(3)
+    z_forward(2)
     stage4(0)
     project(0, 1 - xl, True)
     for half, buf in ((1, B), (0, A)):
@@ -314,32 +351,33 @@
         return buf.at[t, c // 2, pl.ds(c % 2 * 128, 128), :]
 
     def stop(buf, k, c):
-        return buf.at[k, pl.ds(c % 2 * 128, 128), :]
+        return buf.at[k, c // 2, pl.ds(c % 2 * 128, 128), :]
 
     def pass_on(buf, t, u, c, ss, rs, to):
         rc(piece(buf, t, c), piece(buf, u, c), ss, rs.at[u, c], to).start()
 
     def pass_a(j, c):
-        @pl.when(z != 7)
+        around = (z == 7) & (core == 1)
+
+        @pl.when(jnp.logical_not(around))
         def _():
             pass_on(A, j, j + 1, c, s_a.at[0], r_a, nxt)
 
-        @pl.when(z == 7)
+        @pl.when(around)
         def _():
-            to = nxt8 if c < 2 else z0
-            rc(piece(A, j, c), stop(RA, j, c), s_a.at[0], r_d.at[0, j, c % 2], to).start()
+            rc(piece(A, j, c), stop(RA, j, c), s_a.at[0], r_d.at[j, c], nxt8).start()
 
     def pass_b(j, c):
         t = 9 - j
-
-        @pl.when(z != 0)
+        around = (z == 0) & (core == 1)
+
+        @pl.when(jnp.logical_not(around))
         def _():
             pass_on(B, t, t - 1, c, s_b.at[0], r_b, prv)
 
-        @pl.when(z == 0)
+        @pl.when(around)
         def _():
-            to = z7 if c < 2 else prv8
-            rc(piece(B, t, c), stop(RB, j - 1, c), s_b.at[0], r_d.at[1, j - 1, c % 2], to).start()
+            rc(piece(B, t, c), stop(RB, j - 1, c), s_b.at[0], r_d.at[j - 1, c], prv8).start()
 
     def take_a(e):
         j, c = divmod(e, 4)
@@ -355,33 +393,35 @@
         if 1 <= j <= 7:
             pass_b(j, c)
 
-    def help_on(e, here):
+    def help_a(e):
         j, c = divmod(e, 4)
-        if here != (7 if c < 2 else 0):
-            return
         if 0 <= j <= 6:
             ref = stop(RA, j, c)
-            got(ref, r_d.at[0, j, c % 2])
-            to = z0 if c < 2 else nxt8
-            rc(ref, piece(A, j + 1, c), s_d.at[0], r_a.at[j + 1, c], to).start()
+            got(ref, r_d.at[j, c])
+            rc(ref, piece(A, j + 1, c), s_d.at[0], r_a.at[j + 1, c], z0).start()
+
+    def help_b(e):
+        j, c = divmod(e, 4)
         if 1 <= j <= 7:
             ref = stop(RB, j - 1, c)
-            got(ref, r_d.at[1, j - 1, c % 2])
-            to = prv8 if c < 2 else z7
-            rc(ref, piece(B, 8 - j, c), s_d.at[0], r_b.at[8 - j, c], to).start()
+            got(ref, r_d.at[j - 1, c])
+            rc(ref, piece(B, 8 - j, c), s_d.at[0], r_b.at[8 - j, c], z7).start()
 
     def relay(e):
-        @pl.when(z == 0)
-        def _():
-            take_b(e)
-            help_on(e - LAG, 0)
-            take_a(e - LAG)
-
-        @pl.when(z == 7)
-        def _():
-            take_a(e)
-            help_on(e - LAG, 7)
-            take_b(e - LAG)
+        for c in (0, 1):
+            @pl.when((z == 0) & (core == c))
+            def _():
+                take_b(e)
+                if c:
+                    help_b(e - LAGS[2])
+                take_a(e - LAGS[c])
+
+            @pl.when((z == 7) & (core == c))
+            def _():
+                take_a(e)
+                if c:
+                    help_a(e - LAGS[2])
+                take_b(e - LAGS[c])
 
         @pl.when((z > 0) & (z < 4))
         def _():
@@ -437,11 +477,14 @@
                 L[rows, :] += sums
                 O[rows, :] += mixed
 
+    def relay_and(e):
+        relay(e)
+        for action in extra.get(e, ()):
+            action()
+
     def relays(first, last):
         for e in range(first, last):
-            relay(e)
-            for action in extra.get(e, ()):
-                action()
+            relay_and(e)
 
     eighth = [lambda c=c: pass_on(A, 0, 8, c, s_a.at[1], r_a, nxt8) for c in range(4)]
     extra = {
@@ -459,16 +502,16 @@
         24: [lambda: from_below(2, 1)],
         27: [lambda: from_second(2, 1)],
         29: [lambda: from_second(2, 0)],
-        33: [
-            lambda: stage4(2),
-            lambda: send(WO.at[core], WO.at[core], s_m.at[3], r_m.at[3], mate),
-        ],
+        25: [lambda: across(y)],
+        28: [lambda: across(yp)],
+        30: [lambda: across(ym)],
+        34: [lambda: across(y2)],
     }
 
-    relays(LAG, 8)
+    relays(3, 8)
     stage2(1)
 
-    z_got(3)
+    got(z_far(2), r_f.at[2])
     local[4].wait()
     for j in range(0, 16, 2):
         pair = jnp.concatenate([ZO[j].astype(F32), ZO[j + 1].astype(F32)], axis=0)
@@ -476,30 +519,40 @@
 
     gone(SEGW.at[pl.ds(0, 15)], s_m.at[5])
     for p in range(4):
-        gone(z_others(p), s_z.at[p])
+        gone(z_near(p), s_z.at[p])
+    for k in range(3):
+        gone(z_far(k), s_f.at[k])
 
     relays(8, 12)
     stage2_up(1)
     stage3(1)
-    relays(12, 14)
-    project(512, xl, False)
-    relays(14, 16)
-    stage4(1)
-    project(512, 1 - xl, True)
-    for h in (0, 1):
-        for half in (0, 1):
-            rows = pl.ds(half * TOK, TOK)
+    def queries_of(half):
+        rows = pl.ds(half * TOK, TOK)
+        for h in (0, 1):
             low, high = turned(rows, 256 * h)
             dst = pl.ds(h * CHIP + half * TOK, TOK)
             QQ[dst, pl.ds(0, 128)] = low
             QQ[dst, pl.ds(128, 128)] = high
+
+    relays(12, Q_AT - 4)
+    for half in (0, 1):
+        relay_and(Q_AT - 4 + half)
+        project_half(512, xl, False, half)
+    relay_and(Q_AT - 2)
+    stage4(1)
+    project_half(512, 1 - xl, True, 0)
+    queries_of(0)
+    relay_and(Q_AT - 1)
+    project_half(512, 1 - xl, True, 1)
+    queries_of(1)
     got(SEGW.at[pl.ds(0, 16)], r_m.at[2])
 
     todo = [(j, p) for j in range(9) for p in (0, 1)]
-    for e in range(16, 36 + LAG):
+    for e in range(Q_AT, 36 + LAG):
         relays(e, e + 1)
-        if todo and 4 * todo[0][0] + 3 + LAG <= e:
-            attend(*todo.pop(0))
+        for _ in range(1 if e % 2 else 2):
+            if todo and 4 * todo[0][0] + 3 + LAG <= e:
+                attend(*todo.pop(0))
     for j, p in todo:
         attend(j, p)
 
@@ -531,7 +584,7 @@
     got(ATT.at[other], r_m.at[4])
     branch(other, True)
 
-    @pl.loop(0, TOK // 32)
+    @pl.loop(0, TOK // 32, unroll=2)
     def _(i):
         rows = pl.ds(pl.multiple_of(i * 32, 32), 32)
         v = BR[rows, :]
@@ -544,16 +597,17 @@
     for buf, sem in ((A, s_a), (B, s_b)):
         gone(buf.at[pl.ds(0, 7)], sem.at[0])
         gone(buf.at[0], sem.at[1])
-    @pl.when(lax.rem(z, 7) == 0)
+    @pl.when((lax.rem(z, 7) == 0) & (core == 1))
     def _():
         gone(A.at[pl.ds(0, 7)], s_d.at[0])
 
     for stream in range(3):
         streams_gone(stream)
+    gone(WO.at[core], s_m.at[3])
 
 
 def per_device(hidden_in, segment_ids, pre_gain, w_qkv, w_out, post_gain):
-    inverse = 1.0 / 10000.0 ** (jnp.arange(HEAD // 2, dtype=F32) * 2.0 / HEAD)
+    inverse = np.float32(1.0) / np.float32(10000.0) ** (np.arange(HEAD // 2, dtype=np.float32) * 2 / HEAD)
     hbm = pl.BlockSpec(memory_space=pltpu.HBM)
     vmem = pl.BlockSpec(memory_space=pltpu.VMEM)
     dma = pltpu.SemaphoreType.DMA
@@ -581,8 +635,8 @@
             pltpu.VMEM((2 * CHIP, 128), F32),
             pltpu.VMEM((9, 2, TOK, HEAD), BF),
             pltpu.VMEM((9, 2, TOK, HEAD), BF),
-            pltpu.VMEM((7, TOK, HEAD), BF),
-            pltpu.VMEM((7, TOK, HEAD), BF),
+            pltpu.VMEM((7, 2, TOK, HEAD), BF),
+            pltpu.VMEM((7, 2, TOK, HEAD), BF),
             pltpu.VMEM((32, 1, TOK), I32),
             pltpu.VMEM((CHIP, TOK), F32),
             pltpu.VMEM((2, TOK, 512), BF),
@@ -590,11 +644,12 @@
             pltpu.VMEM((TOK, D), F32),
             dma((6,)),
             dma((4,)), dma((4,)),
+            dma((3,)), dma((3,)),
             dma((3,)), dma((3, 6)),
-            dma((3,)), dma((3,)),
+            dma((3,)), dma((6,)),
             dma((2,)), dma((9, 4)),
             dma((2,)), dma((9, 4)),
-            dma((1,)), dma((2, 7, 2)),
+            dma((1,)), dma((7, 4)),
             dma((6,)), dma((6,)),
         ],
         compiler_params=pltpu.CompilerParams(
@@ -605,7 +660,7 @@
         segment_ids,
         w_qkv,
         w_out,
-        inverse.reshape(1, HEAD // 2),
+        jnp.asarray(inverse.astype(np.float32).reshape(1, HEAD // 2)),
         pre_gain.reshape(D // 128, 128),
         post_gain.reshape(D // 128, 128),
     )

time: 114 us -> 105 us (0.921)
  Pallas kernels: 112 us -> 103 us
    pallas_call x1, Pallas kernels: 112 us -> 103 us  [per_device(): pl.pallas_call(kernel, out_shape=pltpu.VMEM((TOK, D), BF), in_specs=[hbm]...]
where the time goes in v3:
time: 105 us; the launch traced here: 104 us
  Pallas kernels  103 us (98%)
    pallas_call x1, Pallas kernels, per_device(): pl.pallas_call(kernel, out_shape=pltpu.VMEM((TOK, D), BF), in_specs=[hbm]...  103 us

profile of v3, /device:TPU:1, one launch (start us, length us, event | category | flops | bytes accessed | tf_op | source)
XLA Modules:
  0.0 104.1 jit_solution(7525341788584343756)
XLA Ops:
  0.0 103.1 %shard_map.73 = bf16[256,2304]{1,0:T(8,128)(2,1)S(1)} custom-call(bf16[256,2304]{1,0:T(8,128)(2,1)} %bitcast.5, s32[1,256]{1,0:T(1,128)} %seg.1, bf16[18,2048]{1,0:T(8,128)(2,1)} %wqkv.1, bf16[8,2304]{1,0:T(8,128)(2,1)} %wout.1, f32[1,128]{1,0:T(1,128)} %constant.2.clone.inverse, f32[18,128]{1,0:T(8,128)} %bitcast.6, f32[18,128]{1,0:T(8,128)} %bitcast.7), custom_call_target="tpu_custom_call" | custom-call | tf_op jit(solution)/shard_map/pallas_call | solution.py:614
  103.1 1.0 copy.9

commit v4 on v3

--- a/solution.py
+++ b/solution.py
@@ -339,8 +339,8 @@
     z_got(3)
     z_forward(2)
     stage4(0)
-    project(0, 1 - xl, True)
-    for half, buf in ((1, B), (0, A)):
+    def own_block(half, buf):
+        project_half(0, 1 - xl, True, half)
         rows = pl.ds(half * TOK, TOK)
         low, high = turned(rows, 0)
         buf[0, 0, :, pl.ds(0, 128)] = low
@@ -381,7 +381,7 @@
 
     def take_a(e):
         j, c = divmod(e, 4)
-        if 1 <= j <= 8:
+        if 1 <= j <= 7:
             got(piece(A, j, c), r_a.at[j, c])
         if 1 <= j <= 6:
             pass_a(j, c)
@@ -433,12 +433,20 @@
             take_a(e)
             take_b(e)
 
+    own_block(1, B)
     for c in range(4):
         pass_on(B, 0, 8, c, s_b.at[1], r_b, nxt8)
+    own_block(0, A)
+    for c in range(4):
         pass_a(0, c)
 
     def attend(j, part):
-        blocks = ((A, 0, 0), (B, 0, 1)) if j == 0 else ((A, j, 0), (B, 9 - j, 1))
+        blocks = (
+            ((A, 0, 0), (B, 0, 1)),
+            *(((A, t, 0), (B, 9 - t, 1)) for t in range(1, 8)),
+            ((B, 1, 1),),
+            ((A, 8, 0),),
+        )[j]
         docs, firsts = [], []
         for _, t, half in blocks:
             index = 16 + 2 * z + half - 2 * t
@@ -488,6 +496,11 @@
 
     eighth = [lambda c=c: pass_on(A, 0, 8, c, s_a.at[1], r_a, nxt8) for c in range(4)]
     extra = {
+        5: [lambda: from_above(1, 1)],
+        7: [lambda: from_above(1, 0)],
+        9: [lambda: from_below(1, 0)],
+        10: [lambda: from_below(1, 1)],
+        13: [lambda: from_second(1, 1), lambda: from_second(1, 0)],
         11: [lambda: to_y(2, y, 0, up, 0)],
         12: [lambda: to_y(2, y, 1, down, 3)],
         14: [lambda: to_y(2, y, 1, up, 1)],
@@ -505,11 +518,11 @@
         25: [lambda: across(y)],
         28: [lambda: across(yp)],
         30: [lambda: across(ym)],
+        31: [lambda: [got(piece(A, 8, c), r_a.at[8, c]) for c in range(4)]],
         34: [lambda: across(y2)],
     }
 
     relays(3, 8)
-    stage2(1)
 
     got(z_far(2), r_f.at[2])
     local[4].wait()
@@ -524,8 +537,6 @@
         gone(z_far(k), s_f.at[k])
 
     relays(8, 12)
-    stage2_up(1)
-    stage3(1)
     def queries_of(half):
         rows = pl.ds(half * TOK, TOK)
         for h in (0, 1):
@@ -547,11 +558,11 @@
     queries_of(1)
     got(SEGW.at[pl.ds(0, 16)], r_m.at[2])
 
-    todo = [(j, p) for j in range(9) for p in (0, 1)]
+    todo = [(j, p) for j in (0, 1, 2, 3, 4, 5, 6, 9, 7, 8) for p in (0, 1)]
     for e in range(Q_AT, 36 + LAG):
         relays(e, e + 1)
         for _ in range(1 if e % 2 else 2):
-            if todo and 4 * todo[0][0] + 3 + LAG <= e:
+            if todo and (31 if todo[0][0] == 9 else 4 * todo[0][0] + 3 + LAG) <= e:
                 attend(*todo.pop(0))
     for j, p in todo:
         attend(j, p)

time: 105 us -> 102 us (0.971)
  Pallas kernels: 103 us -> 101 us
    pallas_call x1, Pallas kernels: 103 us -> 101 us  [per_device(): pl.pallas_call(kernel, out_shape=pltpu.VMEM((TOK, D), BF), in_specs=[hbm]...]
where the time goes in v4:
time: 102 us
  Pallas kernels  101 us (99%)
  local copies, waits for them, and re-layouts  1.02 us (1%)
    pallas_call x1, Pallas kernels, per_device(): pl.pallas_call(kernel, out_shape=pltpu.VMEM((TOK, D), BF), in_specs=[hbm]...  101 us

profile of v4, /device:TPU:1, one launch (start us, length us, event | category | flops | bytes accessed | tf_op | source)
XLA Modules:
  0.0 102.1 jit_solution(11139633474367507000)
XLA Ops:
  0.0 101.1 %shard_map.73 = bf16[256,2304]{1,0:T(8,128)(2,1)S(1)} custom-call(bf16[256,2304]{1,0:T(8,128)(2,1)} %bitcast.5, s32[1,256]{1,0:T(1,128)} %seg.1, bf16[18,2048]{1,0:T(8,128)(2,1)} %wqkv.1, bf16[8,2304]{1,0:T(8,128)(2,1)} %wout.1, f32[1,128]{1,0:T(1,128)} %constant.2.clone.inverse, f32[18,128]{1,0:T(8,128)} %bitcast.6, f32[18,128]{1,0:T(8,128)} %bitcast.7), custom_call_target="tpu_custom_call" | custom-call | tf_op jit(solution)/shard_map/pallas_call | solution.py:625
  101.1 1.0 copy.9

commit v5 on v4

--- a/solution.py
+++ b/solution.py
@@ -20,7 +20,7 @@
 OROWS = 128
 LAGS = (2, 4, 3)
 LAG = max(LAGS)
-Q_AT = 19
+Q_AT = 20
 EPS = 1e-06
 CAP = 50.0
 LOG2E = 1.4426950408889634
@@ -127,7 +127,7 @@
         return rc(src, dst, s_z.at[p], r_z.at[p], to)
 
     def z_send(*pieces):
-        for d in (1, 7, 2, 6):
+        for d in (2, 6, 1, 7):
             for c in (0, 1):
                 for p in pieces:
                     z_copies(p, c, z_dev(d, c)).start()

time: 102 us -> 102 us (level); the launches traced: 102 us -> 101 us
  Pallas kernels: 101 us -> 99.8 us
    pallas_call x1, Pallas kernels: 101 us -> 99.8 us  [per_device(): pl.pallas_call(kernel, out_shape=pltpu.VMEM((TOK, D), BF), in_specs=[hbm]...]
where the time goes in v5:
time: 102 us; the launch traced here: 101 us
  Pallas kernels  99.8 us (98%)
  local copies, waits for them, and re-layouts  1.02 us (1%)
    pallas_call x1, Pallas kernels, per_device(): pl.pallas_call(kernel, out_shape=pltpu.VMEM((TOK, D), BF), in_specs=[hbm]...  99.8 us

profile of v5, /device:TPU:1, one launch (start us, length us, event | category | flops | bytes accessed | tf_op | source)
XLA Modules:
  0.0 100.9 jit_solution(4640673670044135466)
XLA Ops:
  0.0 99.8 %shard_map.73 = bf16[256,2304]{1,0:T(8,128)(2,1)S(1)} custom-call(bf16[256,2304]{1,0:T(8,128)(2,1)} %bitcast.5, s32[1,256]{1,0:T(1,128)} %seg.1, bf16[18,2048]{1,0:T(8,128)(2,1)} %wqkv.1, bf16[8,2304]{1,0:T(8,128)(2,1)} %wout.1, f32[1,128]{1,0:T(1,128)} %constant.2.clone.inverse, f32[18,128]{1,0:T(8,128)} %bitcast.6, f32[18,128]{1,0:T(8,128)} %bitcast.7), custom_call_target="tpu_custom_call" | custom-call | tf_op jit(solution)/shard_map/pallas_call | solution.py:625
  99.9 1.0 %copy.9 = bf16[1,256,2304]{2,1,0:T(8,128)(2,1)} copy(bf16[1,256,2304]{2,1,0:T(8,128)(2,1)S(1)} %bitcast.4) | data formatting | bytes 2359296
